TPU v7x, 32 devices: a whole 2x2x4 slice. The times are simulated.
32 devices in a mesh: dp: 2 (over x), emb: 4 (over z), head: 4 (over y, core).
Axes of the slice: x: 2, y: 2, z: 4, core: 2. Of those that a mesh axis runs over, the one named last changes fastest.
Arguments:
- hidden: bfloat16 [64, 128, 5120], P('dp', None, 'emb'), parts along dimension 0
- g_in: bfloat16 [5120], P('emb')
- w_dq: bfloat16 [5120, 1536], P('emb', 'head')
- g_q: bfloat16 [1536], P('head')
- w_dkv: bfloat16 [5120, 512], P('emb', 'head')
- g_kv: bfloat16 [512], P('head')
- w_kr: bfloat16 [5120, 64], P('emb')
- w_uq: bfloat16 [1536, 128, 192], P(None, 'head')
- w_uk: bfloat16 [512, 128, 128], P(None, 'head')
- w_uv: bfloat16 [512, 128, 128], P(None, 'head')
- w_o: bfloat16 [128, 128, 5120], P('head', None, 'emb')
Outputs:
- output 1: bfloat16 [64, 128, 5120], P('dp', None, 'emb'), parts along dimension 0
- output 2: bfloat16 [64, 128, 512], P('dp', None, 'head'), parts along dimension 0
- output 3: bfloat16 [64, 128, 64], P('dp'), parts along dimension 0
There are 2 independent parts. A program takes and returns all parts, laid end to end along the dimension named above; an argument that names none is the same for every part.
All inputs are finite; a program needn't handle non-finite values.
Results may differ from a plain program's by a relative error of at most 0.02.
Values are sent between devices in bfloat16 or wider.
A program may use at most 1 GiB of HBM per device.

v0:
```python
import math
import jax
import jax.numpy as jnp
from jax import lax
from jax.sharding import PartitionSpec as P

ROPE_BASE = 10000.0
NORM_EPS = 1.0e-6
MSCALE = 0.1 * math.log(40.0) + 1.0


def split_norm(latent, gain_vec, full_width, axis_name):
    wide_vals = latent.astype(jnp.float32)
    sq_sum = lax.psum(jnp.sum(wide_vals * wide_vals, axis=-1, keepdims=True), axis_name)
    return (wide_vals * lax.rsqrt(sq_sum / full_width + NORM_EPS) * gain_vec.astype(jnp.float32)).astype(jnp.bfloat16)


def rope_tables(seq_len, rope_dim):
    half_dim = rope_dim // 2
    inv_freq = ROPE_BASE ** (-2.0 * jnp.arange(half_dim, dtype=jnp.float32) / rope_dim)
    angles = jnp.arange(seq_len, dtype=jnp.float32)[:, None] * inv_freq[None, :]
    return jnp.cos(angles), jnp.sin(angles)


def rotate(values, cos_t, sin_t):
    half_dim = values.shape[-1] // 2
    front_half = values[..., :half_dim]
    back_half = values[..., half_dim:]
    return jnp.concatenate([front_half * cos_t - back_half * sin_t, front_half * sin_t + back_half * cos_t], axis=-1)


def causal_attention(q_nope, q_pe, k_nope, k_pe, v_heads, soft_scale):
    seq_len = q_nope.shape[1]
    q_block = min(seq_len, 128)
    key_pos = jnp.arange(seq_len)

    def attend_block(blk_idx):
        q_start = blk_idx * q_block
        qn_blk = lax.dynamic_slice_in_dim(q_nope, q_start, q_block, axis=1)
        qp_blk = lax.dynamic_slice_in_dim(q_pe, q_start, q_block, axis=1)
        scores = jnp.einsum("hqd,hkd->hqk", qn_blk, k_nope, preferred_element_type=jnp.float32)
        scores = scores + jnp.einsum("hqr,kr->hqk", qp_blk, k_pe, preferred_element_type=jnp.float32)
        q_pos = q_start + jnp.arange(q_block)
        allowed = key_pos[None, :] <= q_pos[:, None]
        scores = jnp.where(allowed, scores * soft_scale, -jnp.inf)
        attn_prob = jax.nn.softmax(scores, axis=-1).astype(jnp.bfloat16)
        return jnp.einsum("irl,ilw->irw", attn_prob, v_heads, preferred_element_type=jnp.float32).astype(jnp.bfloat16)

    return lax.map(attend_block, jnp.arange(seq_len // q_block))


def solution(mesh):
    emb_count = mesh.shape["emb"]
    in_specs = (P("dp", None, "emb"), P("emb"), P("emb", "head"), P("head"), P("emb", "head"), P("head"), P("emb", None), P(None, "head", None), P(None, "head", None), P(None, "head", None), P("head", None, "emb"))
    out_specs = (P("dp", None, "emb"), P("dp", None, "head"), P("dp", None, None))

    def local_block(hidden, g_in, w_dq, g_q, w_dkv, g_kv, w_kr, w_uq, w_uk, w_uv, w_o):
        seq_len = hidden.shape[1]
        nope_dim = w_uk.shape[2]
        soft_scale = MSCALE * MSCALE / math.sqrt(w_uq.shape[2])
        h_norm = split_norm(hidden, g_in, hidden.shape[2] * emb_count, "emb")
        cq_part = jnp.einsum("btd,dc->btc", h_norm, w_dq, preferred_element_type=jnp.float32).astype(jnp.bfloat16)
        ckv_part = jnp.einsum("btd,dc->btc", h_norm, w_dkv, preferred_element_type=jnp.float32).astype(jnp.bfloat16)
        kr_part = jnp.einsum("btd,dc->btc", h_norm, w_kr, preferred_element_type=jnp.float32).astype(jnp.bfloat16)
        c_q, c_kv, k_raw = lax.psum((cq_part, ckv_part, kr_part), "emb")
        cq_loc = split_norm(c_q, g_q, w_uq.shape[0], "head")
        ckv_loc = split_norm(c_kv, g_kv, w_uk.shape[0], "head")
        cq_full = lax.all_gather(cq_loc, "head", axis=2, tiled=True)
        ckv_full = lax.all_gather(ckv_loc, "head", axis=2, tiled=True)
        cos_t, sin_t = rope_tables(seq_len, w_kr.shape[1])
        k_pe = rotate(k_raw.astype(jnp.float32), cos_t, sin_t).astype(jnp.bfloat16)
        wq_nope = w_uq[:, :, :nope_dim]
        wq_rope = w_uq[:, :, nope_dim:]

        def one_seq(seq_in):
            cq_s, ckv_s, kpe_s = seq_in
            q_nope = jnp.einsum("tc,chk->htk", cq_s, wq_nope, preferred_element_type=jnp.float32).astype(jnp.bfloat16)
            q_raw = jnp.einsum("tc,chk->htk", cq_s, wq_rope, preferred_element_type=jnp.float32).astype(jnp.bfloat16)
            q_pe = rotate(q_raw.astype(jnp.float32), cos_t, sin_t).astype(jnp.bfloat16)
            k_nope = jnp.einsum("tc,chk->htk", ckv_s, w_uk, preferred_element_type=jnp.float32).astype(jnp.bfloat16)
            v_heads = jnp.einsum("tc,chk->htk", ckv_s, w_uv, preferred_element_type=jnp.float32).astype(jnp.bfloat16)
            ctx_blocks = causal_attention(q_nope, q_pe, k_nope, kpe_s, v_heads, soft_scale)
            attn_part = jnp.einsum("nhqv,hvd->nqd", ctx_blocks, w_o, preferred_element_type=jnp.float32).astype(jnp.bfloat16)
            return attn_part.reshape(seq_len, w_o.shape[2])

        attn_part = lax.map(one_seq, (cq_full, ckv_full, k_pe))
        attn_sum = lax.psum(attn_part, "head")
        result = (hidden.astype(jnp.float32) + attn_sum.astype(jnp.float32)).astype(jnp.bfloat16)
        return result, ckv_loc, k_pe

    return jax.shard_map(local_block, mesh=mesh, in_specs=in_specs, out_specs=out_specs, check_vma=False)
```

profile of v0, /device:TPU:0, one launch (start us, length us, event | category | flops | bytes accessed | tf_op | source)
XLA Modules:
  0.0 1935.1 jit_solution(6667008852087400097)
XLA Ops:
  13.5 20.5 %psum.49 = f32[32,128,1]{1,0,2:T(8,128)S(1)} all-reduce(f32[32,128,1]{1,0,2:T(8,128)S(1)} %bitcast.108), channel_id=1, replica_groups=mesh['dp'=2,'emb'=4,'head'=4] {'emb'}, use_global_device_ids=true, to_apply=%region_1.0 | all-reduce | flops 4096 | bytes 32768 | tf_op jit(solution)/shard_map/psum | solution.py:14
  34.1 9.8 fusion.74
  52.4 169.2 %all-reduce.7.cloned.1.call-done = (bf16[32,128,384]{2,1,0:T(8,128)(2,1)}, bf16[32,128,128]{2,1,0:T(8,128)(2,1)}, bf16[32,128,64]{1,2,0:T(8,128)(2,1)}) async-done(((bf16[32,128,384]{2,1,0:T(8,128)(2,1)}, bf16[32,128,128]{2,1,0:T(8,128)(2,1)}, bf16[32,128,64]{1,2,0:T(8,128)(2,1)}), (bf16[32,128,384]{2,1,0:T(8,128)(2,1)}, bf16[32,128,128]{2,1,0:T(8,128)(2,1)}, ...) | async-done | bytes 4718608 | tf_op jit(solution)/shard_map/psum | solution.py:65
  226.0 10.7 all-reduce
  242.9 10.8 slice.24
  259.8 16.8 copy.20
  277.9 79.2 %all-gather.3.cloned.1.call-done = bf16[32,128,1536]{2,1,0:T(8,128)(2,1)} async-done(((bf16[32,128,384]{2,1,0:T(8,128)(2,1)}), bf16[32,128,1536]{2,1,0:T(8,128)(2,1)}) %all-gather.3.cloned.1.call-update) | async-done | bytes 12582928 | tf_op jit(solution)/shard_map/all_gather | solution.py:68
  357.2 1370.8 %while.19 = (s32[]{:T(128)}, bf16[32,128,1280]{2,1,0:T(8,128)(2,1)}, bf16[32,128,1536]{2,1,0:T(8,128)(2,1)}, bf16[1536,32,128]{2,1,0:T(8,128)(2,1)}, bf16[32,128...) while((s32[]{:T(128)}, ...), condition=%wide.region_12.13_spmd.clone.clone.clone, body=%wide.region_9.12_spmd.clone.clone.clone.sunk | while | flops 5175959552 | bytes 113724688 | solution.py:86
  365.2 15.8 fusion.138
  392.6 7.4 fusion.140
  408.0 15.8 fusion.138
  435.5 7.4 fusion.140
  450.9 15.8 fusion.138
  478.3 7.4 fusion.140
  493.7 15.8 fusion.138
  536.6 15.8 fusion.138
  564.0 7.4 fusion.140
  579.4 15.8 fusion.138
  606.8 7.4 fusion.140
  622.2 15.8 fusion.138
  649.7 7.4 fusion.140
  665.1 15.8 fusion.138
  707.9 15.8 fusion.138
  735.3 7.4 fusion.140
  750.7 15.8 fusion.138
  778.2 7.4 fusion.140
  793.6 15.8 fusion.138
  821.0 7.4 fusion.140
  836.4 15.8 fusion.138
  863.8 7.4 fusion.140
  879.3 15.8 fusion.138
  906.7 7.4 fusion.140
  922.1 15.8 fusion.138
  949.5 7.4 fusion.140
  964.9 15.8 fusion.138
  1007.8 15.8 fusion.138
  1035.2 7.4 fusion.140
  1050.6 15.8 fusion.138
  1078.0 7.4 fusion.140
  1093.5 15.8 fusion.138
  1120.9 7.4 fusion.140
  1136.3 15.8 fusion.138
  1179.1 15.8 fusion.138
  1206.5 7.4 fusion.140
  1222.0 15.8 fusion.138
  1249.4 7.4 fusion.140
  1264.8 15.8 fusion.138
  1292.2 7.4 fusion.140
  1307.6 15.8 fusion.138
  1350.5 15.8 fusion.138
  1377.9 7.4 fusion.140
  1393.3 15.8 fusion.138
  1420.7 7.4 fusion.140
  1436.2 15.8 fusion.138
  1463.6 7.4 fusion.140
  1479.0 15.8 fusion.138
  1521.8 15.8 fusion.138
  1549.2 7.4 fusion.140
  1564.7 15.8 fusion.138
  1607.5 15.8 fusion.138
  1650.3 15.8 fusion.138
  1693.2 15.8 fusion.138
  1728.0 186.7 %all-reduce.5.cloned.1.call-done = bf16[32,128,1280]{2,1,0:T(8,128)(2,1)} async-done(((bf16[32,128,1280]{2,1,0:T(8,128)(2,1)}), bf16[32,128,1280]{2,1,0:T(8,128)(2,1)}) %all-reduce.5.cloned.1.call-update) | async-done | bytes 10485776 | tf_op jit(solution)/shard_map/psum | solution.py:87
  1914.7 13.8 fusion.64
  (446 shorter events, 735.2 us)
Async XLA Ops:
  7.2 26.9 %copy-start = (bf16[1280,384]{1,0:T(8,128)(2,1)S(1)}, bf16[1280,384]{1,0:T(8,128)(2,1)}, u32[]{:S(2)}) copy-start(bf16[1280,384]{1,0:T(8,128)(2,1)} %param.15) | copy-start | bytes 2949124
  7.2 26.9 %copy-start.4 = (bf16[1280]{0:T(1024)(128)(2,1)S(1)}, bf16[1280]{0:T(1024)(128)(2,1)}, u32[]{:S(2)}) copy-start(bf16[1280]{0:T(1024)(128)(2,1)} %param.14) | copy-start | bytes 7684
  7.2 214.4 %all-reduce.7.cloned.1.call-start = ((), (), s32[]{:S(2)}) async-start(), calls=%async_computation.3 | async-start | bytes 9437184 | tf_op jit(solution)/shard_map/psum | solution.py:65
  7.2 36.7 %slice-start = ((s8[10485760]{0:T(1024)(128)(4,1)}), s8[2097152]{0:T(1024)(128)(4,1)S(1)}, s32[]{:S(2)}) async-start(s8[10485760]{0:T(1024)(128)(4,1)} %bitcast.103), calls=%async_computation.4 | async-start | bytes 4194304
  34.1 9.8 slice-start.1
  34.1 9.8 slice-start.2
  34.1 9.8 copy-start.6
  43.9 4.1 copy-start.7
  48.0 4.4 copy-start.8
  52.3 187.0 %copy-start.5 = (bf16[384]{0:T(512)(128)(2,1)S(1)}, bf16[384]{0:T(512)(128)(2,1)}, u32[]{:S(2)}) copy-start(bf16[384]{0:T(512)(128)(2,1)} %param.16) | copy-start | bytes 2308
  52.3 225.6 %all-gather.5.cloned.1.call-start = ((), (), s32[]{:S(2)}) async-start(), calls=%async_computation.1 | async-start | bytes 5242880 | tf_op jit(solution)/shard_map/all_gather | solution.py:69
  239.3 117.9 %all-gather.3.cloned.1.call-start = ((), (), s32[]{:S(2)}) async-start(), calls=%async_computation | async-start | bytes 15728640 | tf_op jit(solution)/shard_map/all_gather | solution.py:68
  242.9 1671.8 %all-reduce.5.cloned.1.call-start = ((), (), s32[]{:S(2)}) async-start(), calls=%async_computation.2 | async-start | bytes 20971520 | tf_op jit(solution)/shard_map/psum | solution.py:87
  259.8 17.0 copy-start.3
  357.2 8.1 copy-start.2
  400.0 8.1 copy-start.2
  442.8 8.1 copy-start.2
  485.7 8.1 copy-start.2
  528.5 8.1 copy-start.2
  571.3 8.1 copy-start.2
  614.2 8.1 copy-start.2
  657.0 8.1 copy-start.2
  699.9 8.1 copy-start.2
  742.7 8.1 copy-start.2
  785.5 8.1 copy-start.2
  828.4 8.1 copy-start.2
  871.2 8.1 copy-start.2
  914.0 8.1 copy-start.2
  956.9 8.1 copy-start.2
  999.7 8.1 copy-start.2
  1042.6 8.1 copy-start.2
  1085.4 8.1 copy-start.2
  1128.2 8.1 copy-start.2
  1171.1 8.1 copy-start.2
  1213.9 8.1 copy-start.2
  1256.8 8.1 copy-start.2
  1299.6 8.1 copy-start.2
  1342.4 8.1 copy-start.2
  1385.3 8.1 copy-start.2
  1428.1 8.1 copy-start.2
  1470.9 8.1 copy-start.2
  1513.8 8.1 copy-start.2
  1556.6 8.1 copy-start.2
  1599.5 8.1 copy-start.2
  1642.3 8.1 copy-start.2
  1685.1 8.1 copy-start.2
  1914.7 13.8 copy-start.1
Sparse Core Ops, SparseCore 0:
  52.4 169.0 all-reduce.6
  239.4 33.5 all-gather.4
  274.6 82.5 all-gather.2
  1728.1 186.5 all-reduce.4
where the time goes:
time: 1940 us
  matrix products  1310 us (68%)
  waiting for transfers between devices  435 us (22%)
  local copies, waits for them, and re-layouts  88.8 us (5%)
  other arithmetic  56.7 us (3%)
  blocking collectives  31.3 us (2%)
    dot_general x32, matrix products, one_seq(): jnp.einsum('tc,chk->htk', cq_s, wq_nope, preferred_element_type=jnp.float32)  505 us
    dot_general x32, matrix products, one_seq(): jnp.einsum('nhqv,hvd->nqd', ctx_blocks, w_o, preferred_element_type=jnp.f...  236 us
    psum x1, waiting for transfers between devices, local_block(): attn_sum = lax.psum(attn_part, 'head')  187 us
    dot_general x32, matrix products, attend_block(): jnp.einsum('hqd,hkd->hqk', qn_blk, k_nope, preferred_element_type=jnp.flo...  178 us
    psum x1, waiting for transfers between devices, local_block(): c_q, c_kv, k_raw = lax.psum((cq_part, ckv_part, kr_part), 'emb')  169 us
    while x32, matrix products  156 us
    dot_general x32, matrix products, one_seq(): jnp.einsum('tc,chk->htk', ckv_s, w_uv, preferred_element_type=jnp.float32)  126 us
    dot_general x32, matrix products, attend_block(): jnp.einsum('hqr,kr->hqk', qp_blk, k_pe, preferred_element_type=jnp.float32)  89.7 us
  transfers between devices with their start and end apart: 4, of which 3 were waited for; matrix products, arithmetic and copies ran while one was open for 2% of the time, Pallas kernels for 0%

commit v1 on v0

v1 whole, which is shorter than its diff:
```python
import functools
import math
import jax
import jax.numpy as jnp
from jax import lax
from jax.experimental import pallas as pl
from jax.experimental.pallas import tpu as pltpu
from jax.sharding import PartitionSpec as P

ROPE_BASE = 10000.0
NORM_EPS = 1.0e-6
MSCALE = 0.1 * math.log(40.0) + 1.0
LOG2E = math.log2(math.e)
GH = 4
BS = 4
NT = (((1,), (1,)), ((), ()))


def split_norm(latent, gain_vec, full_width, axis_name):
    wide_vals = latent.astype(jnp.float32)
    sq_sum = lax.psum(jnp.sum(wide_vals * wide_vals, axis=-1, keepdims=True), axis_name)
    return (wide_vals * lax.rsqrt(sq_sum / full_width + NORM_EPS) * gain_vec.astype(jnp.float32)).astype(jnp.bfloat16)


def rope_tables(seq_len, rope_dim):
    half_dim = rope_dim // 2
    inv_freq = ROPE_BASE ** (-2.0 * jnp.arange(half_dim, dtype=jnp.float32) / rope_dim)
    angles = jnp.arange(seq_len, dtype=jnp.float32)[:, None] * inv_freq[None, :]
    return jnp.cos(angles), jnp.sin(angles)


def rotate(values, cos_t, sin_t):
    half_dim = values.shape[-1] // 2
    front_half = values[..., :half_dim]
    back_half = values[..., half_dim:]
    return jnp.concatenate([front_half * cos_t - back_half * sin_t, front_half * sin_t + back_half * cos_t], axis=-1)


def attn_kernel(scale, cq_ref, ckv_ref, kp_ref, rope_ref, wq_hbm, wkv_hbm, wo_hbm, out_ref, wq, wkv, wo, ctx, wsem, osem):
    first = pl.program_id(0) == 0
    groups = wq.shape[0]
    seq = rope_ref.shape[0]
    toks = cq_ref.shape[0]
    seqs = toks // seq

    @pl.when(first)
    def _():
        for g in range(groups):
            pltpu.make_async_copy(wq_hbm.at[g], wq.at[g], wsem.at[0, g]).start()
            pltpu.make_async_copy(wkv_hbm.at[g], wkv.at[g], wsem.at[1, g]).start()
        pltpu.make_async_copy(wo_hbm, wo, osem).start()

    lane = lax.broadcasted_iota(jnp.int32, (seq, 128), 1)
    low = (lane & 63) < 32
    causal = lax.broadcasted_iota(jnp.int32, (seq, seq), 0) >= lax.broadcasted_iota(jnp.int32, (seq, seq), 1)

    def group(g, carry):
        @pl.when(first)
        def _():
            pltpu.make_async_copy(wq_hbm.at[g], wq.at[g], wsem.at[0, g]).wait()
            pltpu.make_async_copy(wkv_hbm.at[g], wkv.at[g], wsem.at[1, g]).wait()

        q = jnp.dot(cq_ref[...], wq[g], preferred_element_type=jnp.float32).astype(jnp.bfloat16)
        kv = jnp.dot(ckv_ref[...], wkv[g], preferred_element_type=jnp.float32).astype(jnp.bfloat16)
        for s in range(seqs):
            rows = slice(s * seq, (s + 1) * seq)
            cos_t = rope_ref[:, 0:128]
            sin_t = rope_ref[:, 128:256]
            qps = []
            for t in range(GH // 2):
                u = q[rows, GH * 128 + t * 128:GH * 128 + (t + 1) * 128].astype(jnp.float32)
                swapped = jnp.where(low, pltpu.roll(u, 96, 1), pltpu.roll(u, 32, 1))
                qps.append((u * cos_t + swapped * sin_t).astype(jnp.bfloat16))
            for i in range(GH):
                q_cat = jnp.concatenate([q[rows, i * 128:(i + 1) * 128], qps[i // 2]], axis=1)
                k_cat = jnp.concatenate([kv[rows, i * 128:(i + 1) * 128], kp_ref[rows, (i % 2) * 128:(i % 2 + 1) * 128]], axis=1)
                sc = lax.dot_general(q_cat, k_cat, NT, preferred_element_type=jnp.float32)
                sc = jnp.where(causal, sc, -jnp.inf)
                top = jnp.max(sc, axis=1, keepdims=True)
                e = jnp.exp2((sc - top) * (scale * LOG2E))
                p = (e * (1.0 / jnp.sum(e, axis=1, keepdims=True))).astype(jnp.bfloat16)
                o = jnp.dot(p, kv[rows, (GH + i) * 128:(GH + i + 1) * 128], preferred_element_type=jnp.float32)
                ctx[pl.ds(s * seq, seq), pl.ds(pl.multiple_of(g * (GH * 128) + i * 128, 128), 128)] = o.astype(jnp.bfloat16)
        return carry

    lax.fori_loop(0, groups, group, 0)

    @pl.when(first)
    def _():
        pltpu.make_async_copy(wo_hbm, wo, osem).wait()

    out_ref[...] = jnp.dot(ctx[...], wo[...], preferred_element_type=jnp.float32).astype(jnp.bfloat16)


def attention(cq, ckv, kp, rope, wq, wkv, wo, scale, seq):
    toks, cq_dim = cq.shape
    width = wo.shape[1]
    block = BS * seq
    whole = lambda: pl.BlockSpec(memory_space=pl.ANY)
    return pl.pallas_call(
        functools.partial(attn_kernel, scale),
        grid=(toks // block,),
        out_shape=jax.ShapeDtypeStruct((toks, width), jnp.bfloat16),
        in_specs=[
            pl.BlockSpec((block, cq_dim), lambda b: (b, 0)),
            pl.BlockSpec((block, ckv.shape[1]), lambda b: (b, 0)),
            pl.BlockSpec((block, kp.shape[1]), lambda b: (b, 0)),
            pl.BlockSpec(rope.shape, lambda b: (0, 0)),
            whole(), whole(), whole(),
        ],
        out_specs=pl.BlockSpec((block, width), lambda b: (b, 0)),
        scratch_shapes=[
            pltpu.VMEM(wq.shape, jnp.bfloat16),
            pltpu.VMEM(wkv.shape, jnp.bfloat16),
            pltpu.VMEM(wo.shape, jnp.bfloat16),
            pltpu.VMEM((block, wo.shape[0]), jnp.bfloat16),
            pltpu.SemaphoreType.DMA((2, wq.shape[0])),
            pltpu.SemaphoreType.DMA,
        ],
        compiler_params=pltpu.CompilerParams(dimension_semantics=("arbitrary",), vmem_limit_bytes=67_000_000),
        cost_estimate=pl.CostEstimate(flops=171_000_000_000, bytes_accessed=70_000_000, transcendentals=17_000_000),
        name="mla_attention",
    )(cq, ckv, kp, rope, wq, wkv, wo)


def pack_weights(w_uq, w_uk, w_uv, w_o):
    cdim, heads, qk = w_uq.shape
    nope = w_uk.shape[2]
    groups = heads // GH
    qn = w_uq[:, :, :nope].reshape(cdim, groups, GH * nope)
    qr = w_uq[:, :, nope:].reshape(cdim, groups, GH * (qk - nope))
    wq = jnp.concatenate([qn, qr], axis=2).transpose(1, 0, 2)
    k = w_uk.reshape(w_uk.shape[0], groups, GH * nope)
    v = w_uv.reshape(w_uv.shape[0], groups, GH * w_uv.shape[2])
    wkv = jnp.concatenate([k, v], axis=2).transpose(1, 0, 2)
    return wq, wkv, w_o.reshape(heads * w_o.shape[1], w_o.shape[2])


def solution(mesh):
    emb_count = mesh.shape["emb"]
    in_specs = (P("dp", None, "emb"), P("emb"), P("emb", "head"), P("head"), P("emb", "head"), P("head"), P("emb", None), P(None, "head", None), P(None, "head", None), P(None, "head", None), P("head", None, "emb"))
    out_specs = (P("dp", None, "emb"), P("dp", None, "head"), P("dp", None, None))

    def local_block(hidden, g_in, w_dq, g_q, w_dkv, g_kv, w_kr, w_uq, w_uk, w_uv, w_o):
        nseq, seq_len = hidden.shape[:2]
        soft_scale = MSCALE * MSCALE / math.sqrt(w_uq.shape[2])
        h_norm = split_norm(hidden, g_in, hidden.shape[2] * emb_count, "emb")
        cq_part = jnp.einsum("btd,dc->btc", h_norm, w_dq, preferred_element_type=jnp.float32).astype(jnp.bfloat16)
        ckv_part = jnp.einsum("btd,dc->btc", h_norm, w_dkv, preferred_element_type=jnp.float32).astype(jnp.bfloat16)
        kr_part = jnp.einsum("btd,dc->btc", h_norm, w_kr, preferred_element_type=jnp.float32).astype(jnp.bfloat16)
        c_q, c_kv, k_raw = lax.psum((cq_part, ckv_part, kr_part), "emb")
        cq_loc = split_norm(c_q, g_q, w_uq.shape[0], "head")
        ckv_loc = split_norm(c_kv, g_kv, w_uk.shape[0], "head")
        cq_full = lax.all_gather(cq_loc, "head", axis=2, tiled=True)
        ckv_full = lax.all_gather(ckv_loc, "head", axis=2, tiled=True)
        cos_t, sin_t = rope_tables(seq_len, w_kr.shape[1])
        k_pe = rotate(k_raw.astype(jnp.float32), cos_t, sin_t).astype(jnp.bfloat16)
        rope = jnp.concatenate([jnp.tile(cos_t, (1, 4)), jnp.tile(jnp.concatenate([-sin_t, sin_t], axis=1), (1, 2))], axis=1)
        zeros = jnp.zeros_like(k_pe)
        kp = jnp.concatenate([k_pe, zeros, zeros, k_pe], axis=2)
        wq, wkv, wo = pack_weights(w_uq, w_uk, w_uv, w_o)
        toks = nseq * seq_len
        attn_part = attention(
            cq_full.reshape(toks, -1), ckv_full.reshape(toks, -1), kp.reshape(toks, -1), rope, wq, wkv, wo, soft_scale, seq_len
        )
        attn_sum = lax.psum(attn_part.reshape(hidden.shape), "head")
        result = (hidden.astype(jnp.float32) + attn_sum.astype(jnp.float32)).astype(jnp.bfloat16)
        return result, ckv_loc, k_pe

    return jax.shard_map(local_block, mesh=mesh, in_specs=in_specs, out_specs=out_specs, check_vma=False)
```

time: 1940 us -> 963 us (0.50)
  matrix products: 1310 us -> 18.2 us
  Pallas kernels: 0 us -> 397 us
  waiting for transfers between devices: 435 us -> 367 us
    dot_general x160 -> x0, matrix products: 1130 us -> none  [the longest x32 505 us: one_seq(): jnp.einsum('tc,chk->htk', cq_s, wq_nope, preferred_element_type=jnp.float32)]
    pallas_call x0 -> x1, Pallas kernels: none -> 397 us  [attention(): pl.pallas_call(functools.partial(attn_kernel, scale), grid=(toks // block...]
    while x32 -> x0, matrix products: 156 us -> none
    all_gather x1, waiting for transfers between devices: 79.2 us -> 13.1 us  [local_block(): cq_full = lax.all_gather(cq_loc, 'head', axis=2, tiled=True)]
    dot_general x32 -> x0, local copies, waits for them, and re-layouts: 55 us -> none  [one_seq(): jnp.einsum('tc,chk->htk', ckv_s, w_uv, preferred_element_type=jnp.float32)]
    reshape x0 -> x4, local copies, waits for them, and re-layouts: none -> 38.3 us  [the longest x1 16.7 us: pack_weights(): qn = w_uq[:, :, :nope].reshape(cdim, groups, GH * nope)]
    transpose x0 -> x2, other arithmetic: none -> 23.8 us  [the longest x1 16 us: pack_weights(): wq = jnp.concatenate([qn, qr], axis=2).transpose(1, 0, 2)]
  transfers between devices with their start and end apart: 4 -> 4, of which waited for: 3 -> 3; matrix products, arithmetic and copies ran while one was open for 2% -> 11% of each run, Pallas kernels for 0% -> 0%
where the time goes in v1:
time: 963 us; the launch traced here: 961 us
  Pallas kernels  397 us (41%)
  waiting for transfers between devices  367 us (38%)
  local copies, waits for them, and re-layouts  77 us (8%)
  other arithmetic  56.2 us (6%)
  blocking collectives  31.3 us (3%)
  matrix products  18.2 us (2%)
  between operations  14.1 us (1%)
    pallas_call x1, Pallas kernels, attention(): pl.pallas_call(functools.partial(attn_kernel, scale), grid=(toks // block...  397 us
    psum x1, waiting for transfers between devices, local_block(): attn_sum = lax.psum(attn_part.reshape(hidden.shape), 'head')  185 us
    psum x1, waiting for transfers between devices, local_block(): c_q, c_kv, k_raw = lax.psum((cq_part, ckv_part, kr_part), 'emb')  169 us
    psum x2, blocking collectives, split_norm(): lax.psum(jnp.sum(wide_vals * wide_vals, axis=-1, keepdims=True), axis_name)  31.3 us
  transfers between devices with their start and end apart: 4, of which 3 were waited for; matrix products, arithmetic and copies ran while one was open for 11% of the time, Pallas kernels for 0%

profile of v1, /device:TPU:0, one launch (start us, length us, event | category | flops | bytes accessed | tf_op | source)
XLA Modules:
  0.0 961.3 jit_solution(3628682449689792815)
XLA Ops:
  7.2 0.0 copy-start.5
  7.2 0.0 copy-start.7
  7.2 0.0 all-reduce.7.cloned.1.call-start
  7.2 0.0 slice-start
  7.2 6.2 fusion
  13.5 20.5 %psum.49 = f32[32,128,1]{1,0,2:T(8,128)S(1)} all-reduce(f32[32,128,1]{1,0,2:T(8,128)S(1)} %bitcast.49), channel_id=1, replica_groups=mesh['dp'=2,'emb'=4,'head'=4] {'emb'}, use_global_device_ids=true, to_apply=%region_1.0 | all-reduce | flops 4096 | bytes 32768 | tf_op jit(solution)/shard_map/psum | solution.py:21
  34.0 0.0 copy-done.5
  34.1 0.0 copy-done.7
  34.1 0.0 slice-start.1
  34.1 0.0 slice-start.2
  34.1 0.0 copy-start.8
  34.1 9.8 %fusion.13 = bf16[32,128,384]{2,1,0:T(8,128)(2,1)} fusion(bf16[32,128,1280]{2,1,0:T(8,128)(2,1)} %param.11, f32[1280]{0:T(1024)S(1)} %convert_element_type.50, f32[32,128]{1,0:T(8,128)S(1)} %rsqrt_bitcast_fusion.2, bf16[1280,384]{1,0:T(8,128)(2,1)S(1)} %copy-done.7), kind=kOutput, calls=%fused_computation.19 | convolution fusion | flops 4049076224 | bytes 14636032 | tf_op jit(solution)/shard_map/btd,dc->btc/dot_general | solution.py:148
  43.9 0.0 slice-done
  43.9 0.0 slice-done.1
  43.9 0.0 slice-done.2
  43.9 0.0 copy-done.8
  43.9 0.0 copy-start.9
  43.9 4.1 fusion.19
  48.0 0.0 copy-done.9
  48.0 4.3 fusion.22
  52.3 0.0 all-reduce.7.cloned.1.call-update
  52.3 0.0 all-gather.5.cloned.1.call-start
  52.4 0.0 copy-done.10
  52.4 169.2 %all-reduce.7.cloned.1.call-done = (bf16[32,128,384]{2,1,0:T(8,128)(2,1)}, bf16[32,128,128]{2,1,0:T(8,128)(2,1)}, bf16[32,128,64]{1,2,0:T(8,128)(2,1)}) async-done(((bf16[32,128,384]{2,1,0:T(8,128)(2,1)}, bf16[32,128,128]{2,1,0:T(8,128)(2,1)}, bf16[32,128,64]{1,2,0:T(8,128)(2,1)}), (bf16[32,128,384]{2,1,0:T(8,128)(2,1)}, bf16[32,128,128]{2,1,0:T(8,128)(2,1)}, ...) | async-done | bytes 4718608 | tf_op jit(solution)/shard_map/psum | solution.py:151
  221.6 2.6 fusion.4
  224.2 1.8 fusion.16
  226.0 10.7 %all-reduce = (f32[32,128,1]{1,0,2:T(8,128)S(1)}, f32[32,128,1]{1,0,2:T(8,128)S(1)}) all-reduce(f32[32,128,1]{1,0,2:T(8,128)S(1)} %bitcast.47, f32[32,128,1]{1,0,2:T(8,128)S(1)} %bitcast.48), channel_id=1, replica_groups=mesh['dp'=2,'emb'=4,'head'=4] {'head'}, use_global_device_ids=true, to_apply=%region_4.0 | all-reduce | flops 8192 | bytes 65536 | tf_op jit(solution)/shard_map/psum | solution.py:21
  236.8 2.5 fusion.18
  239.3 0.0 all-gather.5.cloned.1.call-update
  239.3 0.0 all-gather.3.cloned.1.call-start
  239.4 3.5 fusion.6
  242.9 0.0 all-gather.3.cloned.1.call-update
  242.9 0.2 all-reduce.5.cloned.1.call-start
  243.2 10.8 %slice.14 = bf16[1536,32,128]{0,2,1:T(8,128)(2,1)} slice(bf16[1536,32,192]{0,2,1:T(8,128)(2,1)} %param.18), slice={[0:1536], [0:32], [0:128]} | slice | bytes 25165824 | tf_op jit(solution)/shard_map/slice | solution.py:130
  253.9 6.1 slice.15
  260.1 0.1 fusion.30
  260.3 0.1 copy.21
  260.4 0.1 copy.20
  260.5 16.7 %copy.22 = bf16[1536,8,512]{2,0,1:T(8,128)(2,1)} copy(bf16[1536,8,512]{0,2,1:T(8,128)(2,1)} %bitcast.34) | data formatting | bytes 25165824 | tf_op jit(solution)/shard_map/reshape | solution.py:130
  277.2 8.6 copy.23
  285.8 7.5 copy.24
  293.3 6.5 copy.26
  299.8 7.5 copy.25
  307.3 6.4 copy.27
  313.7 0.7 pad_maximum_fusion.1.rope_ref
  314.4 7.9 maximum_bitcast_fusion.1.wkv_hbm
  322.2 16.0 %maximum_bitcast_fusion.wq_hbm = bf16[8,1536,768]{2,1,0:T(8,128)(2,1)} fusion(bf16[1536,8,256]{2,0,1:T(8,128)(2,1)} %copy.23, bf16[1536,8,512]{2,0,1:T(8,128)(2,1)} %copy.22), kind=kLoop, calls=%fused_computation.7 | loop fusion | flops 37748736 | bytes 37748736 | tf_op jit(solution)/shard_map/transpose | solution.py:132
  338.2 0.1 convert_element_type.61
  338.3 0.1 add_convert_fusion
  338.5 0.0 copy-start
  338.5 0.5 copy.18
  339.0 0.2 copy-done.2
  339.2 0.5 copy.19
  339.7 0.1 concatenate.33
  339.8 4.3 concatenate.34.kp_ref
  344.1 13.1 %all-gather.3.cloned.1.call-done = bf16[32,128,1536]{2,1,0:T(8,128)(2,1)} async-done(((bf16[32,128,384]{2,1,0:T(8,128)(2,1)}), bf16[32,128,1536]{2,1,0:T(8,128)(2,1)}) %all-gather.3.cloned.1.call-update) | async-done | bytes 12582928 | tf_op jit(solution)/shard_map/all_gather | solution.py:154
  357.2 397.1 %mla_attention.1 = bf16[4096,1280]{1,0:T(8,128)(2,1)} custom-call(bf16[4096,1536]{1,0:T(8,128)(2,1)} %bitcast.50, bf16[4096,512]{1,0:T(8,128)(2,1)} %bitcast.52, bf16[4096,256]{1,0:T(8,128)(2,1)} %concatenate.34.kp_ref, f32[128,256]{1,0:T(8,128)} %pad_maximum_fusion.1.rope_ref, bf16[8,1536,768]{2,1,0:T(8,128)(2,1)} %maximum_bitcast_fusion.wq_hbm, ...), custom_call_target="tpu_custom_call" | custom-call | flops 171000004608 | bytes 70000000 | tf_op jit(solution)/shard_map/mla_attention/pallas_call | solution.py:100
  754.3 0.0 copy-start.1
  754.3 0.0 all-reduce.5.cloned.1.call-update
  754.3 0.9 copy-done.1
  755.3 0.1 copy-done.3
  755.3 0.9 pad_maximum_fusion
  756.2 184.8 %all-reduce.5.cloned.1.call-done = bf16[32,128,1280]{2,1,0:T(8,128)(2,1)} async-done(((bf16[32,128,1280]{2,1,0:T(8,128)(2,1)}), bf16[32,128,1280]{2,1,0:T(8,128)(2,1)}) %all-reduce.5.cloned.1.call-update) | async-done | bytes 10485776 | tf_op jit(solution)/shard_map/psum | solution.py:166
  941.0 13.8 %fusion.3 = bf16[32,128,1280]{2,1,0:T(8,128)(2,1)} fusion(bf16[32,128,1280]{2,1,0:T(8,128)(2,1)} %param.11, bf16[32,128,1280]{2,1,0:T(8,128)(2,1)} %all-reduce.5.cloned.1.call-done), kind=kLoop, calls=%fused_computation.6 | loop fusion | flops 20971520 | bytes 31457280 | tf_op jit(solution)/shard_map/convert_element_type | solution.py:167
  (20 shorter events, 0.1 us)
Async XLA Ops:
  7.2 26.9 %copy-start.5 = (bf16[1280]{0:T(1024)(128)(2,1)S(1)}, bf16[1280]{0:T(1024)(128)(2,1)}, u32[]{:S(2)}) copy-start(bf16[1280]{0:T(1024)(128)(2,1)} %param.12) | copy-start | bytes 7684
  7.2 26.9 %copy-start.7 = (bf16[1280,384]{1,0:T(8,128)(2,1)S(1)}, bf16[1280,384]{1,0:T(8,128)(2,1)}, u32[]{:S(2)}) copy-start(bf16[1280,384]{1,0:T(8,128)(2,1)} %param.13) | copy-start | bytes 2949124
  7.2 214.4 %all-reduce.7.cloned.1.call-start = ((), (), s32[]{:S(2)}) async-start(), calls=%async_computation.3 | async-start | bytes 9437184 | tf_op jit(solution)/shard_map/psum | solution.py:151
  7.2 36.7 %slice-start = ((s8[10485760]{0:T(1024)(128)(4,1)}), s8[2097152]{0:T(1024)(128)(4,1)S(1)}, s32[]{:S(2)}) async-start(s8[10485760]{0:T(1024)(128)(4,1)} %bitcast.35), calls=%async_computation.4 | async-start | bytes 4194304
  34.1 9.8 %slice-start.1 = ((s8[10485760]{0:T(1024)(128)(4,1)}), s8[4194304]{0:T(1024)(128)(4,1)S(1)}, s32[]{:S(2)}) async-start(s8[10485760]{0:T(1024)(128)(4,1)} %bitcast.35), calls=%async_computation.5 | async-start | bytes 8388608
  34.1 9.8 %slice-start.2 = ((s8[10485760]{0:T(1024)(128)(4,1)}), s8[4194304]{0:T(1024)(128)(4,1)S(1)}, s32[]{:S(2)}) async-start(s8[10485760]{0:T(1024)(128)(4,1)} %bitcast.35), calls=%async_computation.6 | async-start | bytes 8388608
  34.1 9.8 %copy-start.8 = (bf16[1280,128]{1,0:T(8,128)(2,1)S(1)}, bf16[1280,128]{1,0:T(8,128)(2,1)}, u32[]{:S(2)}) copy-start(bf16[1280,128]{1,0:T(8,128)(2,1)} %param.15) | copy-start | bytes 983044
  43.9 4.1 copy-start.9
  48.0 4.4 copy-start.10
  52.3 187.1 %copy-start.6 = (bf16[384]{0:T(512)(128)(2,1)S(1)}, bf16[384]{0:T(512)(128)(2,1)}, u32[]{:S(2)}) copy-start(bf16[384]{0:T(512)(128)(2,1)} %param.14) | copy-start | bytes 2308
  52.3 291.8 %all-gather.5.cloned.1.call-start = ((), (), s32[]{:S(2)}) async-start(), calls=%async_computation.1 | async-start | bytes 5242880 | tf_op jit(solution)/shard_map/all_gather | solution.py:155
  239.3 117.9 %all-gather.3.cloned.1.call-start = ((), (), s32[]{:S(2)}) async-start(), calls=%async_computation | async-start | bytes 15728640 | tf_op jit(solution)/shard_map/all_gather | solution.py:154
  242.9 698.1 %all-reduce.5.cloned.1.call-start = ((), (), s32[]{:S(2)}) async-start(), calls=%async_computation.2 | async-start | bytes 20971520 | tf_op jit(solution)/shard_map/psum | solution.py:166
  322.2 16.0 %copy-start.4 = (bf16[32,128,64]{1,2,0:T(8,128)(2,1)S(1)}, bf16[32,128,64]{1,2,0:T(8,128)(2,1)}, u32[]{:S(2)}) copy-start(bf16[32,128,64]{1,2,0:T(8,128)(2,1)} %get-tuple-element.7) | copy-start | bytes 1572868
  338.5 0.7 copy-start.2
  338.5 1.2 copy-start
  754.3 1.0 copy-start.1
  754.3 1.0 copy-start.3
Sparse Core Ops, SparseCore 0:
  52.5 169.0 all-reduce.6
  239.4 33.5 all-gather.4
  274.6 82.5 all-gather.2
  754.5 186.5 all-reduce.4

commit v2 on v0

v2 whole, which is shorter than its diff:
```python
import functools
import math
import jax
import jax.numpy as jnp
from jax import lax
from jax.experimental import pallas as pl
from jax.experimental.pallas import tpu as pltpu
from jax.sharding import PartitionSpec as P

ROPE_BASE = 10000.0
NORM_EPS = 1.0e-6
MSCALE = 0.1 * math.log(40.0) + 1.0
LOG2E = math.log2(math.e)
GH = 4
BS = 2
LEAD = 5
RING = 8
NT = (((1,), (1,)), ((), ()))
F32 = jnp.float32
BF16 = jnp.bfloat16


def rope_tables(seq_len, rope_dim):
    half_dim = rope_dim // 2
    inv_freq = ROPE_BASE ** (-2.0 * jnp.arange(half_dim, dtype=F32) / rope_dim)
    angles = jnp.arange(seq_len, dtype=F32)[:, None] * inv_freq[None, :]
    return jnp.cos(angles), jnp.sin(angles)


def kernel(
    dims,
    h_hbm, ssq, g_in, gains, rope, rope_t, wd_hbm, wq_hbm, wk_hbm, wv_hbm, wo_hbm,
    out_hbm, ckv_hbm, kpe_hbm, latz, lath,
    wd, wq, wk, wv, wo, qa, ka, va, qb, kb, vb, ctx, cqn, ckvn, lato, latn,
    hbuf, part, rsr, cz, o1s, own, o2s, fin, hres, o1r, o2r, cko, kpo, ssr, gnr, rall,
    wsem, hsem, ssem, gsem, rs_s, rs_r, ag_s, ag_r, ag_l, y_s, y_r, d_s, d_r, f_s, f_r,
    ld, o1_s, o1_r, o2_s, o2_r, o3_s, o3_r, o3_l, hr, cko_l, kpo_l,
):
    nb, seq, nz, d_model, q_lora, kv_lora, scale = dims
    blk = BS * seq
    piece = blk // nz
    groups = wq.shape[0]
    width = h_hbm.shape[1]
    half = width // 2
    qc, kc = q_lora // 4, kv_lora // 4
    lat = qc + kc
    rd = kpe_hbm.shape[1]
    z = lax.axis_index("emb")
    head = lax.axis_index("head")
    core = head % 2
    partner = head + 1 - 2 * core
    ypeer = (head + 2) % 4
    diag = (partner + 2) % 4
    others = (partner, ypeer, diag)

    def remote(src, dst, ss, rs, **where):
        return pltpu.make_async_remote_copy(
            src_ref=src, dst_ref=dst, send_sem=ss, recv_sem=rs, device_id=where, device_id_type=pl.DeviceIdType.MESH
        )

    def rows(b):
        return pl.ds(pl.multiple_of(b * blk, blk), blk)

    def zt(d):
        return (z + d) % nz

    def ss_copy(d):
        return remote(ssq, ssr.at[d - 1], ssem.at[0, d - 1], ssem.at[1, d - 1], emb=zt(d))

    def gn_copy(r):
        return remote(gains, gnr.at[r], gsem.at[0, r], gsem.at[1, r], head=others[r])

    def h_copy(b):
        return pltpu.make_async_copy(h_hbm.at[rows(b)], hbuf.at[b % 2], hsem.at[b % 2])

    def rs_copy(b, d):
        src = part.at[b % 2, pl.ds(pl.multiple_of(zt(d) * piece, piece), piece)]
        return remote(src, rsr.at[b % RING, d - 1], rs_s.at[b, d - 1], rs_r.at[b, d - 1], emb=zt(d))

    def own_rows(b):
        return pl.ds(pl.multiple_of(b * blk + z * piece, piece), piece)

    def ag_copy(b, d):
        return remote(cz.at[b % 2], latz.at[own_rows(b)], ag_s.at[b, d - 1], ag_r.at[b, d - 1], emb=zt(d))

    def ag_local(b):
        return pltpu.make_async_copy(cz.at[b % 2], latz.at[own_rows(b)], ag_l.at[b % 2])

    def y_copy(b):
        return remote(latz.at[rows(b), pl.ds(0, lat)], lath.at[1, rows(b)], y_s.at[b], y_r.at[b], head=ypeer)

    def d_copy(b):
        return remote(latz.at[rows(b), pl.ds(0, lat)], lath.at[0, rows(b)], d_s.at[b], d_r.at[b], head=partner)

    def f_copy(b):
        return remote(lath.at[1, rows(b)], lath.at[2, rows(b)], f_s.at[b], f_r.at[b], head=partner)

    def loads(b):
        return [pltpu.make_async_copy(latz.at[rows(b)], lato, ld.at[0])] + [
            pltpu.make_async_copy(lath.at[r, rows(b)], latn.at[r], ld.at[1 + r]) for r in range(3)
        ]

    def o1_copy(b):
        return remote(o1s.at[b % 2], o1r.at[b % RING], o1_s.at[b], o1_r.at[b], head=partner)

    def o2_copy(b):
        return remote(o2s.at[b % 2], o2r.at[b % RING], o2_s.at[b], o2_r.at[b], head=ypeer)

    def my_half():
        return pl.ds(pl.multiple_of(core * half, half), half)

    def o3_copy(b):
        return remote(fin.at[b % 2], out_hbm.at[rows(b), my_half()], o3_s.at[b], o3_r.at[b], head=partner)

    def o3_local(b):
        return pltpu.make_async_copy(fin.at[b % 2], out_hbm.at[rows(b), my_half()], o3_l.at[b % 2])

    def hr_copy(b):
        return pltpu.make_async_copy(h_hbm.at[rows(b), my_half()], hres.at[b % 2], hr.at[b % 2])

    def cko_copy(b):
        return pltpu.make_async_copy(cko.at[b % 2], ckv_hbm.at[rows(b)], cko_l.at[b % 2])

    def kpo_copy(b):
        return pltpu.make_async_copy(kpo.at[b % 2], kpe_hbm.at[rows(b)], kpo_l.at[b % 2])

    mine = pl.ds(pl.multiple_of(core * half, half), half)
    theirs = pl.ds(pl.multiple_of((1 - core) * half, half), half)
    weight_copies = [
        pltpu.make_async_copy(wd_hbm, wd, wsem.at[0]),
        pltpu.make_async_copy(wq_hbm, wq, wsem.at[1]),
        pltpu.make_async_copy(wk_hbm, wk, wsem.at[2]),
        pltpu.make_async_copy(wv_hbm, wv, wsem.at[3]),
        pltpu.make_async_copy(wo_hbm.at[mine], wo.at[pl.ds(0, half)], wsem.at[4]),
        pltpu.make_async_copy(wo_hbm.at[theirs], wo.at[pl.ds(half, half)], wsem.at[5]),
    ]
    weight_copies[0].start()
    h_copy(0).start()

    barrier = pltpu.get_barrier_semaphore()
    for d in range(1, nz):
        pl.semaphore_signal(barrier, inc=1, device_id={"emb": zt(d)}, device_id_type=pl.DeviceIdType.MESH)
    for other in others:
        pl.semaphore_signal(barrier, inc=1, device_id={"head": other}, device_id_type=pl.DeviceIdType.MESH)
    pl.semaphore_wait(barrier, nz - 1 + 3)

    for d in range(1, nz):
        ss_copy(d).start()
    for r in range(3):
        gn_copy(r).start()
    for copy in weight_copies[1:]:
        copy.start()
    weight_copies[0].wait()
    total = ssq[...]
    for d in range(1, nz):
        ss_copy(d).wait()
        total = total + ssr[d - 1]
    rall[...] = lax.rsqrt(total / d_model + NORM_EPS)

    def down(b):
        h_copy(b).wait()

        @pl.when(b + 1 < nb)
        def _():
            h_copy(b + 1).start()

        @pl.when(b >= 2)
        def _():
            for d in range(1, nz):
                rs_copy(b - 2, d).wait_send()

        for s in range(BS):
            stat = jnp.transpose(jnp.broadcast_to(rall[pl.ds(b * BS + s, 1), :], (seq, seq)))[:, 0:1]
            x = hbuf[b % 2, s * seq:(s + 1) * seq, :].astype(F32)
            hn = (x * stat * g_in[0:1, :]).astype(BF16)
            part[b % 2, s * seq:(s + 1) * seq, :] = jnp.dot(hn, wd[...], preferred_element_type=F32).astype(BF16)
        for d in range(1, nz):
            rs_copy(b, d).start()

    def reduce_z(b):
        for d in range(1, nz):
            rs_copy(b, d).wait_recv()
        acc = part[b % 2, pl.ds(pl.multiple_of(z * piece, piece), piece), :].astype(F32)
        for d in range(1, nz):
            acc = acc + rsr[b % RING, d - 1].astype(F32)

        @pl.when(b >= 2)
        def _():
            for d in range(1, nz):
                ag_copy(b - 2, d).wait_send()

        cz[b % 2] = acc.astype(BF16)
        for d in range(1, nz):
            ag_copy(b, d).start()
        ag_local(b).start()

    def spread(b):
        for d in range(1, nz):
            ag_copy(b, d).wait_recv()
        ag_local(b).wait()
        y_copy(b).start()
        d_copy(b).start()

    def forward(b):
        y_copy(b).wait_recv()
        f_copy(b).start()

    def fetch(b):
        d_copy(b).wait_recv()
        f_copy(b).wait_recv()
        y_copy(b).wait_send()
        d_copy(b).wait_send()
        f_copy(b).wait_send()
        for copy in loads(b):
            copy.start()

    def normalize(b):
        for copy in loads(b):
            copy.wait()

        @pl.when(b >= 2)
        def _():
            cko_copy(b - 2).wait()
            kpo_copy(b - 2).wait()

        @pl.when(b == 0)
        def _():
            for r in range(3):
                gn_copy(r).wait()

        def latent(r, lo, hi):
            return (lato[:, lo:hi] if r == 0 else latn[r - 1, :, lo:hi]).astype(F32)

        def gain(r, lo, hi):
            return gains[0:1, lo:hi] if r == 0 else gnr[r - 1, 0:1, lo:hi]

        order = (head,) + others
        for lo, hi, full, dst in ((0, qc, q_lora, cqn), (qc, lat, kv_lora, ckvn)):
            sq = None
            for r in range(4):
                x = latent(r, lo, hi)
                one = jnp.sum(x * x, axis=1, keepdims=True)
                sq = one if sq is None else sq + one
            stat = lax.rsqrt(sq / full + NORM_EPS)
            for r in range(4):
                y = (latent(r, lo, hi) * stat * gain(r, lo, hi)).astype(BF16)
                dst[:, pl.ds(pl.multiple_of(order[r] * (hi - lo), 128), hi - lo)] = y
                if r == 0 and lo == qc:
                    cko[b % 2] = y
        for s in range(BS):
            u = lato[s * seq:(s + 1) * seq, lat:lat + rd].astype(F32)
            fr, bk = u[:, :rd // 2], u[:, rd // 2:]
            cos_n, sin_n = rope[:, :rd // 2], rope[:, rd // 2:]
            kpo[b % 2, s * seq:(s + 1) * seq, :] = jnp.concatenate(
                [fr * cos_n - bk * sin_n, fr * sin_n + bk * cos_n], axis=1
            ).astype(BF16)
        cko_copy(b).start()
        kpo_copy(b).start()

    causal = lax.broadcasted_iota(jnp.int32, (seq, seq), 0) <= lax.broadcasted_iota(jnp.int32, (seq, seq), 1)

    def project(g, q, k, v):
        q[...] = lax.dot_general(wq[g], cqn[...], NT, preferred_element_type=F32).astype(BF16)
        k[...] = jnp.dot(ckvn[...], wk[g], preferred_element_type=F32).astype(BF16)
        v[...] = lax.dot_general(wv[g], ckvn[...], NT, preferred_element_type=F32).astype(BF16)

    def attend(b, g, q, k, v):
        hr_ = rd // 2
        cos_t, sin_t = rope_t[0:hr_, :], rope_t[hr_:rd, :]
        for s in range(BS):
            cols = slice(s * seq, (s + 1) * seq)
            for i in range(GH):
                base = GH * 128 + i * rd
                fr = q[base:base + hr_, cols].astype(F32)
                bk = q[base + hr_:base + rd, cols].astype(F32)
                q_cat = jnp.concatenate(
                    [q[i * 128:(i + 1) * 128, cols], (fr * cos_t - bk * sin_t).astype(BF16), (fr * sin_t + bk * cos_t).astype(BF16)],
                    axis=0,
                )
                k_cat = jnp.concatenate([k[cols, i * 128:(i + 1) * 128], kpo[b % 2, cols, :]], axis=1)
                sc = jnp.dot(k_cat, q_cat, preferred_element_type=F32)
                sc = jnp.where(causal, sc, -jnp.inf)
                top = jnp.max(sc, axis=0, keepdims=True)
                e = jnp.exp2((sc - top) * (scale * LOG2E))
                p = (e * (1.0 / jnp.sum(e, axis=0, keepdims=True))).astype(BF16)
                o = jnp.dot(v[i * 128:(i + 1) * 128, cols], p, preferred_element_type=F32)
                ctx[pl.ds(pl.multiple_of(g * (GH * 128) + i * 128, 128), 128), cols] = o.astype(BF16)

    def attention(b):
        @pl.when(b == 0)
        def _():
            for copy in weight_copies[1:]:
                copy.wait()

        project(0, qa, ka, va)

        def two(k, carry):
            g = 2 * k
            project(g + 1, qb, kb, vb)
            attend(b, g, qa, ka, va)
            project(g + 2, qa, ka, va)
            attend(b, g + 1, qb, kb, vb)
            return carry

        lax.fori_loop(0, groups // 2 - 1, two, 0)
        project(groups - 1, qb, kb, vb)
        attend(b, groups - 2, qa, ka, va)
        attend(b, groups - 1, qb, kb, vb)

    def out_first(b):
        @pl.when(b >= 2)
        def _():
            o1_copy(b - 2).wait_send()

        o1s[b % 2] = jnp.dot(wo[half:, :], ctx[...], preferred_element_type=F32).astype(BF16)
        o1_copy(b).start()
        own[b % 2] = jnp.dot(wo[:half, :], ctx[...], preferred_element_type=F32)

    def out_second(b):
        o1_copy(b).wait_recv()

        @pl.when(b >= 2)
        def _():
            o2_copy(b - 2).wait_send()

        o2s[b % 2] = (own[b % 2] + o1r[b % RING].astype(F32)).astype(BF16)
        o2_copy(b).start()
        hr_copy(b).start()

    def out_third(b):
        o2_copy(b).wait_recv()
        hr_copy(b).wait()

        @pl.when(b >= 2)
        def _():
            o3_copy(b - 2).wait()
            o3_local(b - 2).wait()

        both = o2s[b % 2].astype(F32) + o2r[b % RING].astype(F32)
        fin[b % 2] = (hres[b % 2].astype(F32) + jnp.transpose(both)).astype(BF16)
        o3_copy(b).start()
        o3_local(b).start()

    def step(n, carry):
        i = n - LEAD

        def stage(fn, b):
            pl.when(jnp.logical_and(b >= 0, b < nb))(lambda: fn(b))

        stage(forward, i + 2)
        stage(spread, i + 3)
        stage(reduce_z, i + 4)
        stage(down, i + 5)
        stage(out_third, i - 2)
        stage(out_second, i - 1)
        stage(normalize, i)
        stage(fetch, i + 1)

        @pl.when(jnp.logical_and(i >= 0, i < nb))
        def _():
            attention(i)
            out_first(i)

        return carry

    lax.fori_loop(0, nb + LEAD + 2, step, 0)

    for b in (nb - 2, nb - 1):
        for d in range(1, nz):
            rs_copy(b, d).wait_send()
            ag_copy(b, d).wait_send()
        o1_copy(b).wait_send()
        o2_copy(b).wait_send()
        o3_copy(b).wait()
        o3_local(b).wait()
        cko_copy(b).wait()
        kpo_copy(b).wait()


def run_kernel(h, ssq, g_in, gains, rope, rope_t, wd, wq, wk, wv, wo, scale, nz, q_lora, kv_lora):
    toks, width = h.shape
    seq = rope.shape[0]
    rd = rope.shape[1]
    nb = toks // (BS * seq)
    blk, half = BS * seq, width // 2
    piece = blk // nz
    lat = q_lora // 4 + kv_lora // 4
    latw = wd.shape[1]
    dims = (nb, seq, nz, width * nz, q_lora, kv_lora, scale)
    dma = lambda *s: pltpu.SemaphoreType.DMA(s)
    vm = lambda *s: pltpu.VMEM(s, BF16)
    vf = lambda *s: pltpu.VMEM(s, F32)
    vmem = pl.BlockSpec(memory_space=pltpu.VMEM)
    anyw = pl.BlockSpec(memory_space=pl.ANY)
    gr = GH * 128
    proj = lambda: [vm(wq.shape[1], blk), vm(blk, gr), vm(gr, blk)]
    shape = jax.ShapeDtypeStruct
    scratch = (
        [vm(*wd.shape), vm(*wq.shape), vm(*wk.shape), vm(*wv.shape), vm(*wo.shape)]
        + proj() + proj()
        + [vm(wo.shape[1], blk), vm(blk, q_lora), vm(blk, kv_lora), vm(blk, latw), vm(3, blk, lat)]
        + [vm(2, blk, width), vm(2, blk, latw), vm(RING, nz - 1, piece, latw), vm(2, piece, latw)]
        + [vm(2, half, blk), vf(2, half, blk), vm(2, half, blk), vm(2, blk, half), vm(2, blk, half)]
        + [vm(RING, half, blk), vm(RING, half, blk), vm(2, blk, kv_lora // 4), vm(2, blk, rd)]
        + [vf(nz - 1, *ssq.shape), vf(3, *gains.shape), vf(*ssq.shape)]
        + [dma(6), dma(2), dma(2, nz - 1), dma(2, 3)]
        + [dma(nb, nz - 1)] * 4 + [dma(2)] + [dma(nb)] * 6
        + [dma(4)] + [dma(nb)] * 6 + [dma(2)] * 4
    )
    return pl.pallas_call(
        functools.partial(kernel, dims),
        out_shape=[
            shape((toks, width), BF16), shape((toks, kv_lora // 4), BF16), shape((toks, rd), BF16),
            shape((toks, latw), BF16), shape((3, toks, lat), BF16),
        ],
        in_specs=[anyw] + [vmem] * 5 + [anyw] * 5,
        out_specs=[anyw] * 5,
        scratch_shapes=scratch,
        compiler_params=pltpu.CompilerParams(collective_id=0, has_side_effects=True, vmem_limit_bytes=67_043_328),
        cost_estimate=pl.CostEstimate(flops=171_000_000_000, bytes_accessed=100_000_000, transcendentals=17_000_000),
        name="mla_block",
    )(h, ssq, g_in, gains, rope, rope_t, wd, wq, wk, wv, wo)


def pack_weights(w_uq, w_uk, w_uv, w_o):
    cdim, heads, qk = w_uq.shape
    kdim, _, nope = w_uk.shape
    groups = heads // GH
    t = w_uq.transpose(1, 2, 0).reshape(groups, GH, qk, cdim)
    wq = jnp.concatenate(
        [t[:, :, :nope].reshape(groups, GH * nope, cdim), t[:, :, nope:].reshape(groups, GH * (qk - nope), cdim)], axis=1
    )
    wk = w_uk.reshape(kdim, groups, GH * nope).transpose(1, 0, 2)
    wv = w_uv.transpose(1, 2, 0).reshape(groups, GH * w_uv.shape[2], kdim)
    wo = w_o.reshape(heads * w_o.shape[1], w_o.shape[2]).T
    return wq, wk, wv, wo


def solution(mesh):
    nz = mesh.shape["emb"]
    in_specs = (P("dp", None, "emb"), P("emb"), P("emb", "head"), P("head"), P("emb", "head"), P("head"), P("emb", None), P(None, "head", None), P(None, "head", None), P(None, "head", None), P("head", None, "emb"))
    out_specs = (P("dp", None, "emb"), P("dp", None, "head"), P("dp", None, None))

    def local_block(hidden, g_in, w_dq, g_q, w_dkv, g_kv, w_kr, w_uq, w_uk, w_uv, w_o):
        nseq, seq, width = hidden.shape
        rd = w_kr.shape[1]
        soft_scale = MSCALE * MSCALE / math.sqrt(w_uq.shape[2])
        wide = hidden.astype(F32)
        ssq = jnp.sum(wide * wide, axis=-1)
        cos_t, sin_t = rope_tables(seq, rd)
        rope = jnp.concatenate([cos_t, sin_t], axis=1)
        gains = jnp.broadcast_to(jnp.concatenate([g_q, g_kv]).astype(F32)[None, :], (8, g_q.shape[0] + g_kv.shape[0]))
        gin = jnp.broadcast_to(g_in.astype(F32)[None, :], (8, width))
        wd = jnp.concatenate([w_dq, w_dkv, w_kr, jnp.zeros((width, 128 - rd), BF16)], axis=1)
        wq, wk, wv, wo = pack_weights(w_uq, w_uk, w_uv, w_o)
        toks = nseq * seq
        out, ckv, kpe = run_kernel(
            hidden.reshape(toks, width), ssq, gin, gains, rope, rope.T, wd, wq, wk, wv, wo,
            soft_scale, nz, w_uq.shape[0], w_uk.shape[0],
        )[:3]
        return out.reshape(hidden.shape), ckv.reshape(nseq, seq, -1), kpe.reshape(nseq, seq, rd)

    return jax.shard_map(local_block, mesh=mesh, in_specs=in_specs, out_specs=out_specs, check_vma=False)
```

time: 1940 us -> 574 us (0.30)
  matrix products: 1310 us -> 0 us
  Pallas kernels: 0 us -> 486 us
  waiting for transfers between devices: 435 us -> 0 us
  other arithmetic: 56.7 us -> 22.6 us
  blocking collectives: 31.3 us -> 0 us
  local copies, waits for them, and re-layouts: 88.8 us -> 63.8 us
    dot_general x163 -> x0, matrix products: 1150 us -> none  [the longest x32 505 us: one_seq(): jnp.einsum('tc,chk->htk', cq_s, wq_nope, preferred_element_type=jnp.float32)]
    pallas_call x0 -> x1, Pallas kernels: none -> 486 us  [run_kernel(): pl.pallas_call(functools.partial(kernel, dims), out_shape=[shape((toks, w...]
    psum x2 -> x0, waiting for transfers between devices: 356 us -> none  [the longest x1 187 us: local_block(): attn_sum = lax.psum(attn_part, 'head')]
    while x32 -> x0, matrix products: 156 us -> none
    all_gather x2 -> x0, waiting for transfers between devices: 79.2 us -> none  [the longest x1 79.2 us: local_block(): cq_full = lax.all_gather(cq_loc, 'head', axis=2, tiled=True)]
    dot_general x32 -> x0, local copies, waits for them, and re-layouts: 55 us -> none  [one_seq(): jnp.einsum('tc,chk->htk', ckv_s, w_uv, preferred_element_type=jnp.float32)]
    psum x2 -> x0, blocking collectives: 31.3 us -> none  [split_norm(): lax.psum(jnp.sum(wide_vals * wide_vals, axis=-1, keepdims=True), axis_name)]
    convert_element_type x39 -> x1, other arithmetic: 22.2 us -> 0.81 us  [local_block(): jnp.concatenate([g_q, g_kv]).astype(F32)[None, :]]
  transfers between devices with their start and end apart: 4 -> 0, of which waited for: 3 -> 0; matrix products, arithmetic and copies ran while one was open for 2% -> 0% of each run, Pallas kernels for 0% -> 0%
where the time goes in v2:
time: 574 us; the launch traced here: 573 us
  Pallas kernels  486 us (85%)
  local copies, waits for them, and re-layouts  63.8 us (11%)
  other arithmetic  22.6 us (4%)
    pallas_call x1, Pallas kernels, run_kernel(): pl.pallas_call(functools.partial(kernel, dims), out_shape=[shape((toks, w...  486 us
    unnamed x19, local copies, waits for them, and re-layouts  20.3 us
    reshape x1, local copies, waits for them, and re-layouts, pack_weights(): wo = w_o.reshape(heads * w_o.shape[1], w_o.shape[2]).T  14.5 us
    concatenate x1, other arithmetic, pack_weights(): jnp.concatenate([t[:, :, :nope].reshape(groups, GH * nope, cdim), t[:, :,...  12.8 us

profile of v2, /device:TPU:0, one launch (start us, length us, event | category | flops | bytes accessed | tf_op | source)
XLA Modules:
  0.0 573.1 jit_solution(7754569961121876581)
XLA Ops:
  0.6 0.0 copy-start.3
  0.6 0.0 copy-start.2
  0.7 0.0 copy-start.1
  0.7 0.0 copy-start.4
  0.7 0.1 pad.5.clone
  0.8 0.8 maximum_convert_fusion
  1.6 0.6 broadcast_in_dim.7.gains
  2.2 6.7 %multiply_reduce_fusion.ssq = f32[32,128]{1,0:T(8,128)} fusion(bf16[32,128,1280]{2,1,0:T(8,128)(2,1)} %param.11), kind=kLoop, calls=%fused_computation | loop fusion | flops 15724544 | bytes 10502144 | tf_op jit(solution)/shard_map/reduce_sum | solution.py:449
  8.9 0.1 fusion.1
  9.0 0.6 fusion.2
  9.6 0.0 copy-done.4
  9.6 0.6 broadcast_in_dim.6.g_in
  10.3 0.7 copy.24.rope
  11.0 0.0 copy-done.3
  11.0 0.2 copy.19
  11.2 0.0 copy-done.2
  11.2 0.0 copy-done.1
  11.2 1.5 maximum_maximum_fusion.wd_hbm
  12.8 7.5 %copy.20 = bf16[512,32,128]{0,2,1:T(8,128)(2,1)} copy(bf16[512,32,128]{2,1,0:T(8,128)(2,1)} %param.19) | data formatting | bytes 8388608 | tf_op args[8]
  20.2 6.4 %copy.21 = bf16[512,8,512]{2,0,1:T(8,128)(2,1)} copy(bf16[512,8,512]{0,2,1:T(8,128)(2,1)} %bitcast.23) | data formatting | bytes 8388608 | tf_op jit(solution)/shard_map/reshape | solution.py:433
  26.7 7.6 %copy.22 = bf16[32,128,512]{2,1,0:T(8,128)(2,1)} copy(bf16[32,128,512]{1,0,2:T(8,128)(2,1)} %bitcast.28) | data formatting | bytes 8388608 | tf_op jit(solution)/shard_map/transpose | solution.py:434
  34.2 6.1 %slice.9 = bf16[8,4,64,1536]{3,2,1,0:T(8,128)(2,1)} slice(bf16[8,4,192,1536]{3,2,1,0:T(8,128)(2,1)} %bitcast.21), slice={[0:8], [0:4], [128:192], [0:1536]} | slice | bytes 12582912 | tf_op jit(solution)/shard_map/slice | solution.py:431
  40.4 0.0 slice-start
  40.4 14.5 %copy.26 = bf16[4096,1280]{0,1:T(8,128)(2,1)} copy(bf16[4096,1280]{1,0:T(8,128)(2,1)} %bitcast.24) | data formatting | bytes 20971520 | tf_op jit(solution)/shard_map/reshape | solution.py:435
  54.8 0.0 slice-start.1
  54.8 6.8 %slice.8 = bf16[8,4,128,1536]{3,2,1,0:T(8,128)(2,1)S(1)} slice(bf16[8,4,192,1536]{3,2,1,0:T(8,128)(2,1)} %bitcast.22), slice={[0:8], [0:4], [0:128], [0:1536]} | slice | bytes 25165824 | tf_op jit(solution)/shard_map/slice | solution.py:431
  61.7 0.0 slice-done
  61.7 0.0 slice-done.1
  61.7 12.8 %pad_maximum_fusion.wq_hbm = bf16[8,768,1536]{2,1,0:T(8,128)(2,1)} fusion(bf16[8,256,1536]{2,1,0:T(8,128)(2,1)S(1)} %bitcast.20, bf16[8,512,1536]{2,1,0:T(8,128)(2,1)S(1)} %bitcast.17), kind=kLoop, calls=%fused_computation.1 | loop fusion | flops 37748736 | bytes 37748736 | tf_op jit(solution)/shard_map/concatenate | solution.py:430
  74.5 486.0 %mla_block.1 = (bf16[4096,1280]{1,0:T(8,128)(2,1)}, bf16[4096,128]{1,0:T(8,128)(2,1)}, bf16[4096,64]{1,0:T(8,128)(2,1)}, bf16[4096,640]{1,0:T(8,128)(2,1)}, bf16[3,4096,512]{2,1,0:T(8,128)(2,1)}) custom-call(bf16[4096,1280]{1,0:T(8,128)(2,1)} %bitcast.25, f32[32,128]{1,0:T(8,128)} %multiply_reduce_fusion.ssq, f32[8,1280]{1,0:T(8,128)} %broadcast_in_dim.6.g_in, ...), custom_call_target="tpu_custom_call" | custom-call | flops 171000004608 | bytes 100000000 | tf_op jit(solution)/shard_map/mla_block/pallas_call | solution.py:410
  560.5 2.3 copy.25
  562.9 0.0 copy-start
  562.9 9.3 %copy.29 = bf16[32,128,1280]{2,1,0:T(8,128)(2,1)} copy(bf16[32,128,1280]{2,1,0:T(8,128)(2,1)} %bitcast.27) | data formatting | bytes 20971520
  572.1 0.0 copy-done
  572.1 1.0 copy.30
  (3 shorter events, 0.0 us)
Async XLA Ops:
  0.6 10.4 %copy-start.3 = (bf16[1280,64]{0,1:T(8,128)(2,1)S(1)}, bf16[1280,64]{0,1:T(8,128)(2,1)}, u32[]{:S(2)}) copy-start(bf16[1280,64]{0,1:T(8,128)(2,1)} %param.17) | copy-start | bytes 491524
  0.6 10.6 %copy-start.2 = (bf16[1280,128]{1,0:T(8,128)(2,1)S(1)}, bf16[1280,128]{1,0:T(8,128)(2,1)}, u32[]{:S(2)}) copy-start(bf16[1280,128]{1,0:T(8,128)(2,1)} %param.15) | copy-start | bytes 983044
  0.7 10.6 %copy-start.1 = (bf16[1280,384]{1,0:T(8,128)(2,1)S(1)}, bf16[1280,384]{1,0:T(8,128)(2,1)}, u32[]{:S(2)}) copy-start(bf16[1280,384]{1,0:T(8,128)(2,1)} %param.13) | copy-start | bytes 2949124
  0.7 9.0 %copy-start.4 = (bf16[1280]{0:T(1024)(128)(2,1)S(1)}, bf16[1280]{0:T(1024)(128)(2,1)}, u32[]{:S(2)}) copy-start(bf16[1280]{0:T(1024)(128)(2,1)} %param.12) | copy-start | bytes 7684
  40.4 21.3 %slice-start = ((s8[6291456]{0:T(1024)(128)(4,1)}), s8[2097152]{0:T(1024)(128)(4,1)S(1)}, s32[]{:S(2)}) async-start(s8[6291456]{0:T(1024)(128)(4,1)} %bitcast.18), calls=%async_computation | async-start | bytes 4194304
  54.8 6.9 %slice-start.1 = ((s8[6291456]{0:T(1024)(128)(4,1)}), s8[4194304]{0:T(1024)(128)(4,1)S(1)}, s32[]{:S(2)}) async-start(s8[6291456]{0:T(1024)(128)(4,1)} %bitcast.18), calls=%async_computation.1 | async-start | bytes 8388608
  562.9 9.3 %copy-start = (bf16[4096,128]{1,0:T(8,128)(2,1)S(1)}, bf16[4096,128]{1,0:T(8,128)(2,1)}, u32[]{:S(2)}) copy-start(bf16[4096,128]{1,0:T(8,128)(2,1)} %get-tuple-element.7) | copy-start | bytes 3145732

commit v3 on v2

--- a/solution.py
+++ b/solution.py
@@ -13,7 +13,7 @@
 LOG2E = math.log2(math.e)
 GH = 4
 BS = 2
-LEAD = 5
+LEAD = 3
 RING = 8
 NT = (((1,), (1,)), ((), ()))
 F32 = jnp.float32
@@ -31,7 +31,7 @@
     dims,
     h_hbm, ssq, g_in, gains, rope, rope_t, wd_hbm, wq_hbm, wk_hbm, wv_hbm, wo_hbm,
     out_hbm, ckv_hbm, kpe_hbm, latz, lath,
-    wd, wq, wk, wv, wo, qa, ka, va, qb, kb, vb, ctx, cqn, ckvn, lato, latn,
+    wd, wq, wk, wv, wo, qa, ka, va, qb, kb, vb, scores, probs, ctx, cqn, ckvn, lato, latn,
     hbuf, part, rsr, cz, o1s, own, o2s, fin, hres, o1r, o2r, cko, kpo, ssr, gnr, rall,
     wsem, hsem, ssem, gsem, rs_s, rs_r, ag_s, ag_r, ag_l, y_s, y_r, d_s, d_r, f_s, f_r,
     ld, o1_s, o1_r, o2_s, o2_r, o3_s, o3_r, o3_l, hr, cko_l, kpo_l,
@@ -261,32 +261,39 @@
 
     def project(g, q, k, v):
         q[...] = lax.dot_general(wq[g], cqn[...], NT, preferred_element_type=F32).astype(BF16)
-        k[...] = jnp.dot(ckvn[...], wk[g], preferred_element_type=F32).astype(BF16)
+        k[...] = lax.dot_general(ckvn[...], wk[g], NT, preferred_element_type=F32).astype(BF16)
         v[...] = lax.dot_general(wv[g], ckvn[...], NT, preferred_element_type=F32).astype(BF16)
 
+    def score(b, u, q, k):
+        cols, i, hd = slice(u // GH * seq, (u // GH + 1) * seq), u % GH, rd // 2
+        cos_t, sin_t = rope_t[0:hd, :], rope_t[hd:rd, :]
+        base = i * (128 + rd)
+        fr = q[base + 128:base + 128 + hd, cols].astype(F32)
+        bk = q[base + 128 + hd:base + 128 + rd, cols].astype(F32)
+        q_cat = jnp.concatenate(
+            [q[base:base + 128, cols], (fr * cos_t - bk * sin_t).astype(BF16), (fr * sin_t + bk * cos_t).astype(BF16)], axis=0
+        )
+        k_cat = jnp.concatenate([k[cols, i * 128:(i + 1) * 128], kpo[b % 2, cols, :]], axis=1)
+        return jnp.dot(k_cat, q_cat, preferred_element_type=F32)
+
+    def softmax(sc):
+        sc = jnp.where(causal, sc, -jnp.inf)
+        top = jnp.max(sc, axis=0, keepdims=True)
+        e = jnp.exp2((sc - top) * (scale * LOG2E))
+        return (e * (1.0 / jnp.sum(e, axis=0, keepdims=True))).astype(BF16)
+
     def attend(b, g, q, k, v):
-        hr_ = rd // 2
-        cos_t, sin_t = rope_t[0:hr_, :], rope_t[hr_:rd, :]
-        for s in range(BS):
-            cols = slice(s * seq, (s + 1) * seq)
-            for i in range(GH):
-                base = GH * 128 + i * rd
-                fr = q[base:base + hr_, cols].astype(F32)
-                bk = q[base + hr_:base + rd, cols].astype(F32)
-                q_cat = jnp.concatenate(
-                    [q[i * 128:(i + 1) * 128, cols], (fr * cos_t - bk * sin_t).astype(BF16), (fr * sin_t + bk * cos_t).astype(BF16)],
-                    axis=0,
-                )
-                k_cat = jnp.concatenate([k[cols, i * 128:(i + 1) * 128], kpo[b % 2, cols, :]], axis=1)
-                sc = jnp.dot(k_cat, q_cat, preferred_element_type=F32)
-                sc = jnp.where(causal, sc, -jnp.inf)
-                top = jnp.max(sc, axis=0, keepdims=True)
-                e = jnp.exp2((sc - top) * (scale * LOG2E))
-                p = (e * (1.0 / jnp.sum(e, axis=0, keepdims=True))).astype(BF16)
-                o = jnp.dot(v[i * 128:(i + 1) * 128, cols], p, preferred_element_type=F32)
-                ctx[pl.ds(pl.multiple_of(g * (GH * 128) + i * 128, 128), 128), cols] = o.astype(BF16)
-
-    def attention(b):
+        units = range(GH * BS)
+        for u in units:
+            scores[u] = score(b, u, q, k)
+        for u in units:
+            probs[u] = softmax(scores[u])
+        for u in units:
+            cols, i = slice(u // GH * seq, (u // GH + 1) * seq), u % GH
+            o = jnp.dot(v[i * 128:(i + 1) * 128, cols], probs[u], preferred_element_type=F32)
+            ctx[pl.ds(pl.multiple_of(g * (GH * 128) + i * 128, 128), 128), cols] = o.astype(BF16)
+
+    def begin(b):
         @pl.when(b == 0)
         def _():
             for copy in weight_copies[1:]:
@@ -294,18 +301,18 @@
 
         project(0, qa, ka, va)
 
-        def two(k, carry):
-            g = 2 * k
-            project(g + 1, qb, kb, vb)
-            attend(b, g, qa, ka, va)
-            project(g + 2, qa, ka, va)
-            attend(b, g + 1, qb, kb, vb)
-            return carry
-
-        lax.fori_loop(0, groups // 2 - 1, two, 0)
+    def two(b, j):
+        g = 2 * j
+        project(g + 1, qb, kb, vb)
+        attend(b, g, qa, ka, va)
+        project(g + 2, qa, ka, va)
+        attend(b, g + 1, qb, kb, vb)
+
+    def finish(b):
         project(groups - 1, qb, kb, vb)
         attend(b, groups - 2, qa, ka, va)
         attend(b, groups - 1, qb, kb, vb)
+        out_first(b)
 
     def out_first(b):
         @pl.when(b >= 2)
@@ -347,20 +354,30 @@
         def stage(fn, b):
             pl.when(jnp.logical_and(b >= 0, b < nb))(lambda: fn(b))
 
-        stage(forward, i + 2)
-        stage(spread, i + 3)
-        stage(reduce_z, i + 4)
-        stage(down, i + 5)
-        stage(out_third, i - 2)
-        stage(out_second, i - 1)
+        active = jnp.logical_and(i >= 0, i < nb)
+        stage(spread, i + 1)
+        stage(reduce_z, i + 2)
+        stage(down, i + 3)
         stage(normalize, i)
-        stage(fetch, i + 1)
-
-        @pl.when(jnp.logical_and(i >= 0, i < nb))
-        def _():
-            attention(i)
-            out_first(i)
-
+        pl.when(active)(lambda: begin(i))
+
+        def pair(j, c):
+            pl.when(active)(lambda: two(i, j))
+
+            @pl.when(j == 0)
+            def _():
+                stage(forward, i + 1)
+                stage(out_third, i - 2)
+                stage(out_second, i - 1)
+
+            @pl.when(j == groups // 2 - 2)
+            def _():
+                stage(fetch, i + 1)
+
+            return c
+
+        lax.fori_loop(0, groups // 2 - 1, pair, 0)
+        pl.when(active)(lambda: finish(i))
         return carry
 
     lax.fori_loop(0, nb + LEAD + 2, step, 0)
@@ -397,7 +414,7 @@
     shape = jax.ShapeDtypeStruct
     scratch = (
         [vm(*wd.shape), vm(*wq.shape), vm(*wk.shape), vm(*wv.shape), vm(*wo.shape)]
-        + proj() + proj()
+        + proj() + proj() + [vf(GH * BS, seq, seq), vm(GH * BS, seq, seq)]
         + [vm(wo.shape[1], blk), vm(blk, q_lora), vm(blk, kv_lora), vm(blk, latw), vm(3, blk, lat)]
         + [vm(2, blk, width), vm(2, blk, latw), vm(RING, nz - 1, piece, latw), vm(2, piece, latw)]
         + [vm(2, half, blk), vf(2, half, blk), vm(2, half, blk), vm(2, blk, half), vm(2, blk, half)]
@@ -426,11 +443,8 @@
     cdim, heads, qk = w_uq.shape
     kdim, _, nope = w_uk.shape
     groups = heads // GH
-    t = w_uq.transpose(1, 2, 0).reshape(groups, GH, qk, cdim)
-    wq = jnp.concatenate(
-        [t[:, :, :nope].reshape(groups, GH * nope, cdim), t[:, :, nope:].reshape(groups, GH * (qk - nope), cdim)], axis=1
-    )
-    wk = w_uk.reshape(kdim, groups, GH * nope).transpose(1, 0, 2)
+    wq = w_uq.transpose(1, 2, 0).reshape(groups, GH * qk, cdim)
+    wk = w_uk.transpose(1, 2, 0).reshape(groups, GH * nope, kdim)
     wv = w_uv.transpose(1, 2, 0).reshape(groups, GH * w_uv.shape[2], kdim)
     wo = w_o.reshape(heads * w_o.shape[1], w_o.shape[2]).T
     return wq, wk, wv, wo

time: 574 us -> 442 us (0.77); the launches traced: 573 us -> 435 us
  Pallas kernels: 486 us -> 380 us
  local copies, waits for them, and re-layouts: 63.8 us -> 44.4 us
  other arithmetic: 22.6 us -> 9.82 us
    pallas_call x1, Pallas kernels: 486 us -> 380 us  [run_kernel(): pl.pallas_call(functools.partial(kernel, dims), out_shape=[shape((toks, w...]
    slice x2 -> x0, local copies, waits for them, and re-layouts: 13 us -> none  [the longest x1 6.85 us: pack_weights(): t[:, :, :nope].reshape(groups, GH * nope, cdim)]
    concatenate x1 -> x0, other arithmetic: 12.8 us -> none  [pack_weights(): jnp.concatenate([t[:, :, :nope].reshape(groups, GH * nope, cdim), t[:, :,...]
    transpose x0 -> x1, local copies, waits for them, and re-layouts: none -> 7.59 us  [pack_weights(): wk = w_uk.transpose(1, 2, 0).reshape(groups, GH * nope, kdim)]
    unnamed x19 -> x14, local copies, waits for them, and re-layouts: 20.3 us -> 12.8 us
    reshape x1 -> x0, local copies, waits for them, and re-layouts: 6.45 us -> none  [pack_weights(): wk = w_uk.reshape(kdim, groups, GH * nope).transpose(1, 0, 2)]
where the time goes in v3:
time: 442 us; the launch traced here: 435 us
  Pallas kernels  380 us (86%)
  local copies, waits for them, and re-layouts  44.4 us (10%)
  other arithmetic  9.82 us (2%)
    pallas_call x1, Pallas kernels, run_kernel(): pl.pallas_call(functools.partial(kernel, dims), out_shape=[shape((toks, w...  380 us
    reshape x1, local copies, waits for them, and re-layouts, pack_weights(): wo = w_o.reshape(heads * w_o.shape[1], w_o.shape[2]).T  14.3 us
    unnamed x14, local copies, waits for them, and re-layouts  12.8 us

profile of v3, /device:TPU:0, one launch (start us, length us, event | category | flops | bytes accessed | tf_op | source)
XLA Modules:
  0.0 434.7 jit_solution(8157176288985379622)
XLA Ops:
  0.7 0.1 pad.3.clone
  0.7 0.7 maximum_convert_fusion
  1.4 0.6 broadcast_in_dim.7.gains
  2.0 0.0 copy-start.4
  2.0 0.0 copy-start.3
  2.0 0.0 copy-start.1
  2.0 0.0 copy-start.2
  2.0 6.8 %multiply_reduce_fusion.ssq = f32[32,128]{1,0:T(8,128)} fusion(bf16[32,128,1280]{2,1,0:T(8,128)(2,1)} %param.11), kind=kLoop, calls=%fused_computation | loop fusion | flops 15724544 | bytes 10502144 | tf_op jit(solution)/shard_map/reduce_sum | solution.py:463
  8.9 0.1 fusion.1
  9.0 0.6 fusion.2
  9.6 0.0 copy-done.4
  9.6 0.6 broadcast_in_dim.6.g_in
  10.2 0.7 copy.18.rope
  11.0 0.0 copy-done.3
  11.0 0.2 copy.14
  11.2 0.0 copy-done.1
  11.2 0.0 copy-done.2
  11.2 1.5 maximum_maximum_fusion.wd_hbm
  12.8 7.6 %copy.15 = bf16[32,128,512]{2,1,0:T(8,128)(2,1)} copy(bf16[32,128,512]{1,0,2:T(8,128)(2,1)} %bitcast.19) | data formatting | bytes 8388608 | tf_op jit(solution)/shard_map/transpose | solution.py:447
  20.3 7.6 %copy.16 = bf16[32,128,512]{2,1,0:T(8,128)(2,1)} copy(bf16[32,128,512]{1,0,2:T(8,128)(2,1)} %bitcast.20) | data formatting | bytes 8388608 | tf_op jit(solution)/shard_map/transpose | solution.py:448
  27.9 14.3 %copy.20 = bf16[4096,1280]{0,1:T(8,128)(2,1)} copy(bf16[4096,1280]{1,0:T(8,128)(2,1)} %bitcast.15) | data formatting | bytes 20971520 | tf_op jit(solution)/shard_map/reshape | solution.py:449
  42.3 379.8 %mla_block.1 = (bf16[4096,1280]{1,0:T(8,128)(2,1)}, bf16[4096,128]{1,0:T(8,128)(2,1)}, bf16[4096,64]{1,0:T(8,128)(2,1)}, bf16[4096,640]{1,0:T(8,128)(2,1)}, bf16[3,4096,512]{2,1,0:T(8,128)(2,1)}) custom-call(bf16[4096,1280]{1,0:T(8,128)(2,1)} %bitcast.16, f32[32,128]{1,0:T(8,128)} %multiply_reduce_fusion.ssq, f32[8,1280]{1,0:T(8,128)} %broadcast_in_dim.6.g_in, ...), custom_call_target="tpu_custom_call" | custom-call | flops 171000004608 | bytes 100000000 | tf_op jit(solution)/shard_map/mla_block/pallas_call | solution.py:427
  422.1 2.3 copy.19
  424.4 0.0 copy-start
  424.4 9.3 %copy.23 = bf16[32,128,1280]{2,1,0:T(8,128)(2,1)} copy(bf16[32,128,1280]{2,1,0:T(8,128)(2,1)} %bitcast.17) | data formatting | bytes 20971520
  433.7 0.0 copy-done
  433.7 1.0 copy.24
  (2 shorter events, 0.0 us)
Async XLA Ops:
  2.0 7.6 %copy-start.4 = (bf16[1280]{0:T(1024)(128)(2,1)S(1)}, bf16[1280]{0:T(1024)(128)(2,1)}, u32[]{:S(2)}) copy-start(bf16[1280]{0:T(1024)(128)(2,1)} %param.12) | copy-start | bytes 7684
  2.0 8.9 %copy-start.3 = (bf16[1280,64]{0,1:T(8,128)(2,1)S(1)}, bf16[1280,64]{0,1:T(8,128)(2,1)}, u32[]{:S(2)}) copy-start(bf16[1280,64]{0,1:T(8,128)(2,1)} %param.17) | copy-start | bytes 491524
  2.0 9.1 %copy-start.1 = (bf16[1280,384]{1,0:T(8,128)(2,1)S(1)}, bf16[1280,384]{1,0:T(8,128)(2,1)}, u32[]{:S(2)}) copy-start(bf16[1280,384]{1,0:T(8,128)(2,1)} %param.13) | copy-start | bytes 2949124
  2.0 9.2 %copy-start.2 = (bf16[1280,128]{1,0:T(8,128)(2,1)S(1)}, bf16[1280,128]{1,0:T(8,128)(2,1)}, u32[]{:S(2)}) copy-start(bf16[1280,128]{1,0:T(8,128)(2,1)} %param.15) | copy-start | bytes 983044
  424.4 9.3 %copy-start = (bf16[4096,128]{1,0:T(8,128)(2,1)S(1)}, bf16[4096,128]{1,0:T(8,128)(2,1)}, u32[]{:S(2)}) copy-start(bf16[4096,128]{1,0:T(8,128)(2,1)} %get-tuple-element.7) | copy-start | bytes 3145732

commit v4 on v3

--- a/solution.py
+++ b/solution.py
@@ -124,18 +124,27 @@
     def kpo_copy(b):
         return pltpu.make_async_copy(kpo.at[b % 2], kpe_hbm.at[rows(b)], kpo_l.at[b % 2])
 
-    mine = pl.ds(pl.multiple_of(core * half, half), half)
-    theirs = pl.ds(pl.multiple_of((1 - core) * half, half), half)
     weight_copies = [
         pltpu.make_async_copy(wd_hbm, wd, wsem.at[0]),
         pltpu.make_async_copy(wq_hbm, wq, wsem.at[1]),
         pltpu.make_async_copy(wk_hbm, wk, wsem.at[2]),
         pltpu.make_async_copy(wv_hbm, wv, wsem.at[3]),
-        pltpu.make_async_copy(wo_hbm.at[mine], wo.at[pl.ds(0, half)], wsem.at[4]),
-        pltpu.make_async_copy(wo_hbm.at[theirs], wo.at[pl.ds(half, half)], wsem.at[5]),
     ]
+
+    def wo_chunk(j):
+        at = pl.ds(pl.multiple_of((core * half + j * 128) % width, 128), 128)
+        return pltpu.make_async_copy(wo_hbm.at[:, at], ctx.at[:, pl.ds(j % 2 * 128, 128)], wsem.at[4 + j % 2])
+
+    def turn(j):
+        wo_chunk(j).wait()
+        wo[j * 128:(j + 1) * 128, :] = jnp.transpose(ctx[:, j % 2 * 128:(j % 2 + 1) * 128].astype(F32)).astype(BF16)
+        if (j + 2) * 128 < width:
+            wo_chunk(j + 2).start()
+
     weight_copies[0].start()
     h_copy(0).start()
+    wo_chunk(0).start()
+    wo_chunk(1).start()
 
     barrier = pltpu.get_barrier_semaphore()
     for d in range(1, nz):
@@ -169,11 +178,12 @@
             for d in range(1, nz):
                 rs_copy(b - 2, d).wait_send()
 
+        hn = []
         for s in range(BS):
             stat = jnp.transpose(jnp.broadcast_to(rall[pl.ds(b * BS + s, 1), :], (seq, seq)))[:, 0:1]
             x = hbuf[b % 2, s * seq:(s + 1) * seq, :].astype(F32)
-            hn = (x * stat * g_in[0:1, :]).astype(BF16)
-            part[b % 2, s * seq:(s + 1) * seq, :] = jnp.dot(hn, wd[...], preferred_element_type=F32).astype(BF16)
+            hn.append((x * stat * g_in[0:1, :]).astype(BF16))
+        part[b % 2] = jnp.dot(jnp.concatenate(hn, axis=0), wd[...], preferred_element_type=F32).astype(BF16)
         for d in range(1, nz):
             rs_copy(b, d).start()
 
@@ -214,6 +224,8 @@
         for copy in loads(b):
             copy.start()
 
+    front = lax.broadcasted_iota(jnp.int32, (seq, 128), 1) < rd // 2
+
     def normalize(b):
         for copy in loads(b):
             copy.wait()
@@ -236,11 +248,12 @@
 
         order = (head,) + others
         for lo, hi, full, dst in ((0, qc, q_lora, cqn), (qc, lat, kv_lora, ckvn)):
-            sq = None
+            acc = None
             for r in range(4):
-                x = latent(r, lo, hi)
-                one = jnp.sum(x * x, axis=1, keepdims=True)
-                sq = one if sq is None else sq + one
+                for t in range(lo, hi, 128):
+                    x = latent(r, t, t + 128)
+                    acc = x * x if acc is None else acc + x * x
+            sq = jnp.sum(acc, axis=1, keepdims=True)
             stat = lax.rsqrt(sq / full + NORM_EPS)
             for r in range(4):
                 y = (latent(r, lo, hi) * stat * gain(r, lo, hi)).astype(BF16)
@@ -248,12 +261,10 @@
                 if r == 0 and lo == qc:
                     cko[b % 2] = y
         for s in range(BS):
-            u = lato[s * seq:(s + 1) * seq, lat:lat + rd].astype(F32)
-            fr, bk = u[:, :rd // 2], u[:, rd // 2:]
-            cos_n, sin_n = rope[:, :rd // 2], rope[:, rd // 2:]
-            kpo[b % 2, s * seq:(s + 1) * seq, :] = jnp.concatenate(
-                [fr * cos_n - bk * sin_n, fr * sin_n + bk * cos_n], axis=1
-            ).astype(BF16)
+            u = lato[s * seq:(s + 1) * seq, lat:lat + 128].astype(F32)
+            swapped = jnp.where(front, pltpu.roll(u, 128 - rd // 2, 1), pltpu.roll(u, rd // 2, 1))
+            turned = u * rope[:, 0:128] + swapped * rope[:, 128:256]
+            kpo[b % 2, s * seq:(s + 1) * seq, :] = turned[:, :rd].astype(BF16)
         cko_copy(b).start()
         kpo_copy(b).start()
 
@@ -355,9 +366,15 @@
             pl.when(jnp.logical_and(b >= 0, b < nb))(lambda: fn(b))
 
         active = jnp.logical_and(i >= 0, i < nb)
-        stage(spread, i + 1)
         stage(reduce_z, i + 2)
         stage(down, i + 3)
+        chunks = width // 128
+        for m in range(LEAD):
+            @pl.when(n == m)
+            def _():
+                for j in range(chunks * m // LEAD, chunks * (m + 1) // LEAD):
+                    turn(j)
+
         stage(normalize, i)
         pl.when(active)(lambda: begin(i))
 
@@ -373,6 +390,7 @@
             @pl.when(j == groups // 2 - 2)
             def _():
                 stage(fetch, i + 1)
+                stage(spread, i + 2)
 
             return c
 
@@ -396,8 +414,7 @@
 
 def run_kernel(h, ssq, g_in, gains, rope, rope_t, wd, wq, wk, wv, wo, scale, nz, q_lora, kv_lora):
     toks, width = h.shape
-    seq = rope.shape[0]
-    rd = rope.shape[1]
+    seq, rd = rope.shape[0], rope_t.shape[0]
     nb = toks // (BS * seq)
     blk, half = BS * seq, width // 2
     piece = blk // nz
@@ -413,9 +430,9 @@
     proj = lambda: [vm(wq.shape[1], blk), vm(blk, gr), vm(gr, blk)]
     shape = jax.ShapeDtypeStruct
     scratch = (
-        [vm(*wd.shape), vm(*wq.shape), vm(*wk.shape), vm(*wv.shape), vm(*wo.shape)]
+        [vm(*wd.shape), vm(*wq.shape), vm(*wk.shape), vm(*wv.shape), vm(*wo.shape[::-1])]
         + proj() + proj() + [vf(GH * BS, seq, seq), vm(GH * BS, seq, seq)]
-        + [vm(wo.shape[1], blk), vm(blk, q_lora), vm(blk, kv_lora), vm(blk, latw), vm(3, blk, lat)]
+        + [vm(wo.shape[0], blk), vm(blk, q_lora), vm(blk, kv_lora), vm(blk, latw), vm(3, blk, lat)]
         + [vm(2, blk, width), vm(2, blk, latw), vm(RING, nz - 1, piece, latw), vm(2, piece, latw)]
         + [vm(2, half, blk), vf(2, half, blk), vm(2, half, blk), vm(2, blk, half), vm(2, blk, half)]
         + [vm(RING, half, blk), vm(RING, half, blk), vm(2, blk, kv_lora // 4), vm(2, blk, rd)]
@@ -446,7 +463,7 @@
     wq = w_uq.transpose(1, 2, 0).reshape(groups, GH * qk, cdim)
     wk = w_uk.transpose(1, 2, 0).reshape(groups, GH * nope, kdim)
     wv = w_uv.transpose(1, 2, 0).reshape(groups, GH * w_uv.shape[2], kdim)
-    wo = w_o.reshape(heads * w_o.shape[1], w_o.shape[2]).T
+    wo = w_o.reshape(heads * w_o.shape[1], w_o.shape[2])
     return wq, wk, wv, wo
 
 
@@ -462,14 +479,16 @@
         wide = hidden.astype(F32)
         ssq = jnp.sum(wide * wide, axis=-1)
         cos_t, sin_t = rope_tables(seq, rd)
-        rope = jnp.concatenate([cos_t, sin_t], axis=1)
+        pad = jnp.zeros((seq, 128 - rd), F32)
+        rope = jnp.concatenate([cos_t, cos_t, pad, -sin_t, sin_t, pad], axis=1)
+        rope_t = jnp.concatenate([cos_t, sin_t], axis=1).T
         gains = jnp.broadcast_to(jnp.concatenate([g_q, g_kv]).astype(F32)[None, :], (8, g_q.shape[0] + g_kv.shape[0]))
         gin = jnp.broadcast_to(g_in.astype(F32)[None, :], (8, width))
         wd = jnp.concatenate([w_dq, w_dkv, w_kr, jnp.zeros((width, 128 - rd), BF16)], axis=1)
         wq, wk, wv, wo = pack_weights(w_uq, w_uk, w_uv, w_o)
         toks = nseq * seq
         out, ckv, kpe = run_kernel(
-            hidden.reshape(toks, width), ssq, gin, gains, rope, rope.T, wd, wq, wk, wv, wo,
+            hidden.reshape(toks, width), ssq, gin, gains, rope, rope_t, wd, wq, wk, wv, wo,
             soft_scale, nz, w_uq.shape[0], w_uk.shape[0],
         )[:3]
         return out.reshape(hidden.shape), ckv.reshape(nseq, seq, -1), kpe.reshape(nseq, seq, rd)

time: 442 us -> 401 us (0.907); the launches traced: 435 us -> 399 us
  Pallas kernels: 380 us -> 358 us
  local copies, waits for them, and re-layouts: 44.4 us -> 30.3 us
    pallas_call x1, Pallas kernels: 380 us -> 358 us  [run_kernel(): pl.pallas_call(functools.partial(kernel, dims), out_shape=[shape((toks, w...]
    reshape x1 -> x0, local copies, waits for them, and re-layouts: 14.3 us -> none  [pack_weights(): wo = w_o.reshape(heads * w_o.shape[1], w_o.shape[2]).T]
where the time goes in v4:
time: 401 us; the launch traced here: 399 us
  Pallas kernels  358 us (89%)
  local copies, waits for them, and re-layouts  30.3 us (8%)
  other arithmetic  9.8 us (2%)
    pallas_call x1, Pallas kernels, run_kernel(): pl.pallas_call(functools.partial(kernel, dims), out_shape=[shape((toks, w...  358 us
    unnamed x14, local copies, waits for them, and re-layouts  12.8 us

profile of v4, /device:TPU:0, one launch (start us, length us, event | category | flops | bytes accessed | tf_op | source)
XLA Modules:
  0.0 399.2 jit_solution(1709123299303473153)
XLA Ops:
  0.7 0.1 pad.3.clone
  0.7 0.7 maximum_convert_fusion
  1.4 0.6 broadcast_in_dim.9.gains
  2.0 0.0 copy-start.4
  2.0 0.0 copy-start.3
  2.0 0.0 copy-start.1
  2.0 0.0 copy-start.2
  2.0 6.8 %multiply_reduce_fusion.ssq = f32[32,128]{1,0:T(8,128)} fusion(bf16[32,128,1280]{2,1,0:T(8,128)(2,1)} %param.11), kind=kLoop, calls=%fused_computation | loop fusion | flops 15724544 | bytes 10502144 | tf_op jit(solution)/shard_map/reduce_sum | solution.py:480
  8.8 0.0 copy-done.4
  8.8 0.6 broadcast_in_dim.8.g_in
  9.5 0.1 fusion
  9.6 0.6 maximum_bitcast_fusion.rope_t
  10.2 0.1 copy.14
  10.3 0.1 copy.17
  10.4 0.1 copy.16
  10.5 0.8 concatenate.17.rope
  11.3 0.0 copy-done.3
  11.3 0.2 copy.18
  11.6 0.0 copy-done.1
  11.6 0.0 copy-done.2
  11.6 1.5 maximum_maximum_fusion.wd_hbm
  13.1 7.5 %copy.19 = bf16[32,128,512]{2,1,0:T(8,128)(2,1)} copy(bf16[32,128,512]{1,0,2:T(8,128)(2,1)} %bitcast.16) | data formatting | bytes 8388608 | tf_op jit(solution)/shard_map/transpose | solution.py:464
  20.6 7.6 %copy.20 = bf16[32,128,512]{2,1,0:T(8,128)(2,1)} copy(bf16[32,128,512]{1,0,2:T(8,128)(2,1)} %bitcast.17) | data formatting | bytes 8388608 | tf_op jit(solution)/shard_map/transpose | solution.py:465
  28.2 358.4 %mla_block.1 = (bf16[4096,1280]{1,0:T(8,128)(2,1)}, bf16[4096,128]{1,0:T(8,128)(2,1)}, bf16[4096,64]{1,0:T(8,128)(2,1)}, bf16[4096,640]{1,0:T(8,128)(2,1)}, bf16[3,4096,512]{2,1,0:T(8,128)(2,1)}) custom-call(bf16[4096,1280]{1,0:T(8,128)(2,1)} %bitcast.14, f32[32,128]{1,0:T(8,128)} %multiply_reduce_fusion.ssq, f32[8,1280]{1,0:T(8,128)} %broadcast_in_dim.8.g_in, ...), custom_call_target="tpu_custom_call" | custom-call | flops 171000004608 | bytes 100000000 | tf_op jit(solution)/shard_map/mla_block/pallas_call | solution.py:444
  386.6 2.3 copy.21
  389.0 0.0 copy-start
  389.0 9.3 %copy.24 = bf16[32,128,1280]{2,1,0:T(8,128)(2,1)} copy(bf16[32,128,1280]{2,1,0:T(8,128)(2,1)} %bitcast.15) | data formatting | bytes 20971520
  398.2 0.0 copy-done
  398.2 1.0 copy.25
  (3 shorter events, 0.0 us)
Async XLA Ops:
  2.0 6.8 %copy-start.4 = (bf16[1280]{0:T(1024)(128)(2,1)S(1)}, bf16[1280]{0:T(1024)(128)(2,1)}, u32[]{:S(2)}) copy-start(bf16[1280]{0:T(1024)(128)(2,1)} %param.12) | copy-start | bytes 7684
  2.0 9.3 %copy-start.3 = (bf16[1280,64]{0,1:T(8,128)(2,1)S(1)}, bf16[1280,64]{0,1:T(8,128)(2,1)}, u32[]{:S(2)}) copy-start(bf16[1280,64]{0,1:T(8,128)(2,1)} %param.17) | copy-start | bytes 491524
  2.0 9.5 %copy-start.1 = (bf16[1280,384]{1,0:T(8,128)(2,1)S(1)}, bf16[1280,384]{1,0:T(8,128)(2,1)}, u32[]{:S(2)}) copy-start(bf16[1280,384]{1,0:T(8,128)(2,1)} %param.13) | copy-start | bytes 2949124
  2.0 9.5 %copy-start.2 = (bf16[1280,128]{1,0:T(8,128)(2,1)S(1)}, bf16[1280,128]{1,0:T(8,128)(2,1)}, u32[]{:S(2)}) copy-start(bf16[1280,128]{1,0:T(8,128)(2,1)} %param.15) | copy-start | bytes 983044
  389.0 9.3 %copy-start = (bf16[4096,128]{1,0:T(8,128)(2,1)S(1)}, bf16[4096,128]{1,0:T(8,128)(2,1)}, u32[]{:S(2)}) copy-start(bf16[4096,128]{1,0:T(8,128)(2,1)} %get-tuple-element.7) | copy-start | bytes 3145732

commit v5 on v4

--- a/solution.py
+++ b/solution.py
@@ -367,7 +367,8 @@
 
         active = jnp.logical_and(i >= 0, i < nb)
         stage(reduce_z, i + 2)
-        stage(down, i + 3)
+        pl.when(i <= 0)(lambda: stage(down, i + LEAD))
+        pl.when(jnp.logical_and(i >= 0, i + LEAD + 1 < nb))(lambda: down(i + LEAD + 1))
         chunks = width // 128
         for m in range(LEAD):
             @pl.when(n == m)
@@ -383,9 +384,12 @@
 
             @pl.when(j == 0)
             def _():
-                stage(forward, i + 1)
                 stage(out_third, i - 2)
                 stage(out_second, i - 1)
+
+            @pl.when(j == max(groups // 2 - 3, 0))
+            def _():
+                stage(forward, i + 1)
 
             @pl.when(j == groups // 2 - 2)
             def _():

time: 401 us -> 404 us (level)
  no operation moved by 1% of the time
where the time goes in v5:
time: 404 us; the launch traced here: 401 us
  Pallas kernels  360 us (89%)
  local copies, waits for them, and re-layouts  30.3 us (8%)
  other arithmetic  9.8 us (2%)
    pallas_call x1, Pallas kernels, run_kernel(): pl.pallas_call(functools.partial(kernel, dims), out_shape=[shape((toks, w...  360 us
    unnamed x14, local copies, waits for them, and re-layouts  12.8 us

profile of v5, /device:TPU:0, one launch (start us, length us, event | category | flops | bytes accessed | tf_op | source)
XLA Modules:
  0.0 401.1 jit_solution(10294375998721477186)
XLA Ops:
  0.7 0.1 pad.3.clone
  0.7 0.7 maximum_convert_fusion
  1.4 0.6 broadcast_in_dim.9.gains
  2.0 0.0 copy-start.4
  2.0 0.0 copy-start.3
  2.0 0.0 copy-start.1
  2.0 0.0 copy-start.2
  2.0 6.8 %multiply_reduce_fusion.ssq = f32[32,128]{1,0:T(8,128)} fusion(bf16[32,128,1280]{2,1,0:T(8,128)(2,1)} %param.11), kind=kLoop, calls=%fused_computation | loop fusion | flops 15724544 | bytes 10502144 | tf_op jit(solution)/shard_map/reduce_sum | solution.py:484
  8.8 0.0 copy-done.4
  8.8 0.6 broadcast_in_dim.8.g_in
  9.5 0.1 fusion
  9.6 0.6 maximum_bitcast_fusion.rope_t
  10.2 0.1 copy.14
  10.3 0.1 copy.17
  10.4 0.1 copy.16
  10.5 0.8 concatenate.17.rope
  11.3 0.0 copy-done.3
  11.3 0.2 copy.18
  11.6 0.0 copy-done.1
  11.6 0.0 copy-done.2
  11.6 1.5 maximum_maximum_fusion.wd_hbm
  13.1 7.5 %copy.19 = bf16[32,128,512]{2,1,0:T(8,128)(2,1)} copy(bf16[32,128,512]{1,0,2:T(8,128)(2,1)} %bitcast.16) | data formatting | bytes 8388608 | tf_op jit(solution)/shard_map/transpose | solution.py:468
  20.6 7.6 %copy.20 = bf16[32,128,512]{2,1,0:T(8,128)(2,1)} copy(bf16[32,128,512]{1,0,2:T(8,128)(2,1)} %bitcast.17) | data formatting | bytes 8388608 | tf_op jit(solution)/shard_map/transpose | solution.py:469
  28.2 360.3 %mla_block.1 = (bf16[4096,1280]{1,0:T(8,128)(2,1)}, bf16[4096,128]{1,0:T(8,128)(2,1)}, bf16[4096,64]{1,0:T(8,128)(2,1)}, bf16[4096,640]{1,0:T(8,128)(2,1)}, bf16[3,4096,512]{2,1,0:T(8,128)(2,1)}) custom-call(bf16[4096,1280]{1,0:T(8,128)(2,1)} %bitcast.14, f32[32,128]{1,0:T(8,128)} %multiply_reduce_fusion.ssq, f32[8,1280]{1,0:T(8,128)} %broadcast_in_dim.8.g_in, ...), custom_call_target="tpu_custom_call" | custom-call | flops 171000004608 | bytes 100000000 | tf_op jit(solution)/shard_map/mla_block/pallas_call | solution.py:448
  388.5 2.3 copy.21
  390.9 0.0 copy-start
  390.9 9.3 %copy.24 = bf16[32,128,1280]{2,1,0:T(8,128)(2,1)} copy(bf16[32,128,1280]{2,1,0:T(8,128)(2,1)} %bitcast.15) | data formatting | bytes 20971520
  400.2 0.0 copy-done
  400.2 1.0 copy.25
  (3 shorter events, 0.0 us)
Async XLA Ops:
  2.0 6.8 %copy-start.4 = (bf16[1280]{0:T(1024)(128)(2,1)S(1)}, bf16[1280]{0:T(1024)(128)(2,1)}, u32[]{:S(2)}) copy-start(bf16[1280]{0:T(1024)(128)(2,1)} %param.12) | copy-start | bytes 7684
  2.0 9.3 %copy-start.3 = (bf16[1280,64]{0,1:T(8,128)(2,1)S(1)}, bf16[1280,64]{0,1:T(8,128)(2,1)}, u32[]{:S(2)}) copy-start(bf16[1280,64]{0,1:T(8,128)(2,1)} %param.17) | copy-start | bytes 491524
  2.0 9.5 %copy-start.1 = (bf16[1280,384]{1,0:T(8,128)(2,1)S(1)}, bf16[1280,384]{1,0:T(8,128)(2,1)}, u32[]{:S(2)}) copy-start(bf16[1280,384]{1,0:T(8,128)(2,1)} %param.13) | copy-start | bytes 2949124
  2.0 9.5 %copy-start.2 = (bf16[1280,128]{1,0:T(8,128)(2,1)S(1)}, bf16[1280,128]{1,0:T(8,128)(2,1)}, u32[]{:S(2)}) copy-start(bf16[1280,128]{1,0:T(8,128)(2,1)} %param.15) | copy-start | bytes 983044
  390.9 9.3 %copy-start = (bf16[4096,128]{1,0:T(8,128)(2,1)S(1)}, bf16[4096,128]{1,0:T(8,128)(2,1)}, u32[]{:S(2)}) copy-start(bf16[4096,128]{1,0:T(8,128)(2,1)} %get-tuple-element.7) | copy-start | bytes 3145732
